TPU v7x, 256 devices: a whole 4x4x8 slice. The times are simulated.
256 devices in a mesh: sy: 16 (over y, x), sx: 8 (over z), wl: 2 (over core).
Axes of the slice: x: 4, y: 4, z: 8, core: 2. Of those that a mesh axis runs over, the one named last changes fastest.
Arguments:
- interface_map: bfloat16 [32, 8, 1536, 2, 1536], P(('wl', 'sy'), 'sx'), parts along dimension 0, may hold values from -0.0625 to 0.0625
- source_trace: float32 [32, 8, 2, 64, 4, 384], P(('wl', 'sy'), 'sx'), parts along dimension 0, may hold values from -6 to 6
- restriction: float32 [32, 8, 2, 32, 4, 384], P(('wl', 'sy'), 'sx'), parts along dimension 0, may hold values from -0.009765625 to 0.009765625
- prolongation: float32 [32, 8, 2, 32, 4, 384], P(('wl', 'sy'), 'sx'), parts along dimension 0, may hold values from -0.109375 to 0.109375
- coarse_inverse: float32 [4, 32, 32], P('wl'), parts along dimension 0, may hold values from -0.75 to 0.75
Outputs:
- traces: float32 [32, 8, 2, 64, 4, 384], P(('wl', 'sy'), 'sx'), parts along dimension 0
- coarse_coef: float32 [4, 64, 32], P('wl'), parts along dimension 0
There are 2 independent parts, one for each index of `wl`. A program takes and returns all parts, laid end to end along the dimension named above; each array names one. Nothing has to cross between parts.
All inputs are finite; a program needn't handle non-finite values.
Results may differ from a plain program's by a relative error of at most 0.0025.
Values sent between devices are 32-bit elements; how exact they have to be, the bound alone decides.
A program may use at most 128 MiB of HBM per device.

v0:
```python
import functools

import jax
import jax.numpy as jnp
from jax import lax
from jax.sharding import Mesh
from jax.sharding import PartitionSpec as P

ITERS = 6
SY = ("sy_0", "sy_1")
SY_SX = ("sy_0", "sy_1", "sx")
WL_SY = ("wl", "sy_0", "sy_1")


PRECISE = lax.Precision.HIGHEST


def shifted(value, axis, by):
    peers = lax.axis_size(axis)
    pairs = [(i, i + by) for i in range(peers) if 0 <= i + by < peers]
    return lax.ppermute(value, axis, pairs)


def with_halo(value, sides, width):
    for axis, dim in sides:
        peers, length = (lax.axis_size(axis), value.shape[dim])
        up = [(i, (i + 1) % peers) for i in range(peers - 1)]
        down = [(j, i) for i, j in up]
        last = lax.slice_in_dim(value, length - width, length, axis=dim)
        initial = lax.slice_in_dim(value, 0, width, axis=dim)
        before = lax.ppermute(last, axis, up)
        after = lax.ppermute(initial, axis, down)
        value = jnp.concatenate([before, value, after], axis=dim)
    return value


def over_axes(value, axes):
    return functools.reduce(lax.psum, axes, value)


def complex_pair(left_real, left_imag, right_real, right_imag, pattern):
    real_part = jnp.einsum(pattern, left_real, right_real, precision=PRECISE) - jnp.einsum(
        pattern, left_imag, right_imag, precision=PRECISE
    )
    imag_part = jnp.einsum(pattern, left_real, right_imag, precision=PRECISE) + jnp.einsum(
        pattern, left_imag, right_real, precision=PRECISE
    )
    return jnp.stack([real_part, imag_part])


def corner_values(outgoing):
    corner_northwest = outgoing[..., 0, 0] + outgoing[..., 2, 0]
    corner_northeast = outgoing[..., 0, -1] + outgoing[..., 3, 0]
    corner_southwest = outgoing[..., 1, 0] + outgoing[..., 2, -1]
    corner_southeast = outgoing[..., 1, -1] + outgoing[..., 3, -1]
    return (corner_northwest, corner_northeast, corner_southwest, corner_southeast)


def assemble(
    from_north,
    from_south,
    from_west,
    from_east,
    into_northwest,
    into_northeast,
    into_southwest,
    into_southeast,
):
    north_side = (
        from_north.at[..., 0].add(0.5 * into_northwest).at[..., -1].add(0.5 * into_northeast)
    )
    south_side = (
        from_south.at[..., 0].add(0.5 * into_southwest).at[..., -1].add(0.5 * into_southeast)
    )
    west_side = from_west.at[..., 0].add(0.5 * into_northwest).at[..., -1].add(0.5 * into_southwest)
    east_side = from_east.at[..., 0].add(0.5 * into_northeast).at[..., -1].add(0.5 * into_southeast)
    return jnp.stack([north_side, south_side, west_side, east_side], axis=-2)


def restrict_sum(traces, weights):
    src_count, side_len = (traces.shape[1], traces.shape[3])
    coarse_width = weights.shape[1]
    flat_traces = traces.reshape(2, src_count, 4 * side_len)
    flat_weights = weights.reshape(2, coarse_width, 4 * side_len)
    return complex_pair(
        flat_traces[0], flat_traces[1], flat_weights[0], flat_weights[1], "sk,nk->sn"
    )


def outgoing_traces(traces, map_shard, source_shard):
    src_count, side_len = (traces.shape[1], traces.shape[3])
    row_block = traces.astype(jnp.bfloat16).reshape(2 * src_count, 4 * side_len)
    map_table = map_shard.reshape(4 * side_len, 8 * side_len)
    product = jnp.dot(row_block, map_table, preferred_element_type=jnp.float32).reshape(
        2, src_count, 2, 4 * side_len
    )
    real_part = product[0, :, 0] - product[1, :, 1]
    imag_part = product[0, :, 1] + product[1, :, 0]
    return jnp.stack([real_part, imag_part]).reshape(2, src_count, 4, side_len) + source_shard


def exchange_relayed(outgoing):
    corner_northwest, corner_northeast, corner_southwest, corner_southeast = corner_values(outgoing)
    from_west, west_corners = shifted(
        (outgoing[:, :, 3], jnp.stack([corner_northeast, corner_southeast])), "sx", 1
    )
    from_east, east_corners = shifted(
        (outgoing[:, :, 2], jnp.stack([corner_northwest, corner_southwest])), "sx", -1
    )
    from_north, north_corners = shifted(
        (outgoing[:, :, 1], jnp.stack([west_corners[1], east_corners[1]])), SY, 1
    )
    from_south, south_corners = shifted(
        (outgoing[:, :, 0], jnp.stack([west_corners[0], east_corners[0]])), SY, -1
    )
    return assemble(
        from_north,
        from_south,
        from_west,
        from_east,
        north_corners[0],
        north_corners[1],
        south_corners[0],
        south_corners[1],
    )


def sender_restriction(weights):
    receive_northwest = 0.5 * (weights[:, :, 0, 0] + weights[:, :, 2, 0])
    receive_northeast = 0.5 * (weights[:, :, 0, -1] + weights[:, :, 3, 0])
    receive_southwest = 0.5 * (weights[:, :, 1, 0] + weights[:, :, 2, -1])
    receive_southeast = 0.5 * (weights[:, :, 1, -1] + weights[:, :, 3, -1])
    empty_slot = jnp.zeros_like(weights[:, :, 0])

    def spread_slot(vector):
        return jnp.broadcast_to(vector[:, :, None], empty_slot.shape)

    weight_grid = jnp.stack(
        [
            jnp.stack(
                [spread_slot(receive_northwest), weights[:, :, 0], spread_slot(receive_northeast)]
            ),
            jnp.stack([weights[:, :, 2], empty_slot, weights[:, :, 3]]),
            jnp.stack(
                [spread_slot(receive_southwest), weights[:, :, 1], spread_slot(receive_southeast)]
            ),
        ]
    )
    padded = with_halo(weight_grid, ((SY, 0), ("sx", 1)), 1)
    weight_northwest = padded[0, 0][..., 0]
    weight_northeast = padded[0, 4][..., 0]
    weight_southwest = padded[4, 0][..., 0]
    weight_southeast = padded[4, 4][..., 0]
    north_weights = padded[0, 2].at[..., 0].add(weight_northwest).at[..., -1].add(weight_northeast)
    south_weights = padded[4, 2].at[..., 0].add(weight_southwest).at[..., -1].add(weight_southeast)
    west_weights = padded[2, 0].at[..., 0].add(weight_northwest).at[..., -1].add(weight_southwest)
    east_weights = padded[2, 4].at[..., 0].add(weight_northeast).at[..., -1].add(weight_southeast)
    return jnp.stack([north_weights, south_weights, west_weights, east_weights], axis=2)


def per_device(interface_map, source_trace, restriction, prolongation, coarse_inverse):
    source_shard = source_trace[0, 0]
    weights = restriction[0, 0]
    src_count, side_len = (source_shard.shape[1], source_shard.shape[3])
    coarse_width = weights.shape[1]
    lift_flat = prolongation[0, 0].reshape(2, coarse_width, 4 * side_len)
    traces = jnp.zeros(source_shard.shape, jnp.float32)
    coef_now = jnp.zeros((2, src_count, coarse_width), jnp.float32)
    coarse_total = coef_now
    sender_weights = sender_restriction(weights)
    for sweep_index in range(ITERS):
        coef_now = complex_pair(
            coarse_total[0], coarse_total[1], coarse_inverse[0], coarse_inverse[1], "sn,nq->sq"
        )
        spread = complex_pair(coef_now[0], coef_now[1], lift_flat[0], lift_flat[1], "sn,nk->sk")
        corrected = traces + spread.reshape(traces.shape)
        outgoing = outgoing_traces(corrected, interface_map, source_shard)
        if sweep_index + 1 < ITERS:
            coarse_total = over_axes(restrict_sum(outgoing, sender_weights), SY_SX)
        traces = exchange_relayed(outgoing)
    return (traces[None, None], coef_now)


def solution(mesh):
    finer = Mesh(
        mesh.devices.reshape(4, 4, mesh.shape["sx"], mesh.shape["wl"]), ("sy_0", "sy_1", "sx", "wl")
    )
    return jax.shard_map(
        per_device,
        mesh=finer,
        in_specs=(
            P(WL_SY, "sx", None, None, None),
            P(WL_SY, "sx", None, None, None, None),
            P(WL_SY, "sx", None, None, None, None),
            P(WL_SY, "sx", None, None, None, None),
            P("wl", None, None),
        ),
        out_specs=(P(WL_SY, "sx", None, None, None, None), P("wl", None, None)),
        check_vma=False,
    )
```

profile of v0, /device:TPU:80, one launch (start us, length us, event | category | flops | bytes accessed | tf_op | source)
XLA Modules:
  0.0 676.1 jit_solution(9231777959875446169)
XLA Ops:
  2.5 9.8 %copy.272 = bf16[192,8,2,1536]{3,1,2,0:T(8,128)(2,1)} copy(bf16[192,8,2,1536]{3,2,1,0:T(2,128)(2,1)} %bitcast.727) | data formatting | bytes 18874368
  12.3 12.7 %copy.114 = bf16[3072,1536]{1,0:T(8,128)(2,1)} copy(bf16[3072,1536]{0,1:T(8,128)(2,1)} %bitcast.702) | data formatting | bytes 18874368 | tf_op jit(solution)/shard_map/dot_general | solution.py:94
  27.3 6.8 %fusion.29 = f32[2,64,2,1536]{3,1,2,0:T(8,128)S(1)} fusion(bf16[2,1536,1536,1]{2,1,0,3:T(8,128)(2,1)} %bitcast.696, bf16[1,64,1536]{2,1,0:T(8,128)(2,1)S(1)} %fusion.2, bf16[1,64,1536]{2,1,0:T(8,128)(2,1)S(1)} %fusion.3), kind=kOutput, calls=%fused_computation.106 | convolution fusion | flops 1208745984 | bytes 11403264 | tf_op jit(solution)/shard_map/dot_general | solution.py:94
  40.6 3.8 collective-permute-start.1
  44.4 3.4 collective-permute-start
  47.8 5.1 collective-permute-start.6
  55.6 4.5 collective-permute-start.4
  62.1 5.6 collective-permute-done.3
  76.0 6.0 collective-permute-start.9
  94.5 3.8 collective-permute-start.10
  108.5 7.1 %collective-permute-done.11 = f32[5,1,2,32,384]{4,3,2,1,0:T(8,128)} collective-permute-done((f32[5,1,2,32,384]{4,3,2,1,0:T(8,128)}, f32[5,1,2,32,384]{4,3,2,1,0:T(8,128)}, u32[]{:S(2)}, u32[]{:S(2)}) %collective-permute-start.11) | collective-permute-done | bytes 491552 | tf_op jit(solution)/shard_map/ppermute | solution.py:32
  121.1 15.6 %psum.105 = f32[2,64,32]{1,2,0:T(8,128)S(1)} all-reduce(f32[2,64,32]{1,2,0:T(8,128)S(1)} %pad_maximum_fusion.1), channel_id=1, replica_groups=mesh['sy_0'=4,'sy_1'=4,'sx'=8,'wl'=2] {'sy_0'}, use_global_device_ids=true, to_apply=%region_0.0 | all-reduce | flops 4096 | bytes 32768 | tf_op jit(solution)/shard_map/psum | solution.py:38
  136.7 14.4 %psum.106 = f32[2,64,32]{1,2,0:T(8,128)S(1)} all-reduce(f32[2,64,32]{1,2,0:T(8,128)S(1)} %psum.105), channel_id=1, replica_groups=mesh['sy_0'=4,'sy_1'=4,'sx'=8,'wl'=2] {'sy_1'}, use_global_device_ids=true, to_apply=%region_1.0 | all-reduce | flops 4096 | bytes 32768 | tf_op jit(solution)/shard_map/psum | solution.py:38
  151.1 28.8 %psum.107 = f32[2,64,32]{1,2,0:T(8,128)S(1)} all-reduce(f32[2,64,32]{1,2,0:T(8,128)S(1)} %psum.106), channel_id=1, replica_groups=mesh['sy_0'=4,'sy_1'=4,'sx'=8,'wl'=2] {'sx'}, use_global_device_ids=true, to_apply=%region_2.0 | all-reduce | flops 4096 | bytes 32768 | tf_op jit(solution)/shard_map/psum | solution.py:38
  184.9 6.8 fusion.40
  195.2 14.4 %psum.108 = f32[2,64,32]{1,2,0:T(8,128)S(1)} all-reduce(f32[2,64,32]{1,2,0:T(8,128)S(1)} %pad_maximum_fusion.2), channel_id=1, replica_groups=mesh['sy_0'=4,'sy_1'=4,'sx'=8,'wl'=2] {'sy_0'}, use_global_device_ids=true, to_apply=%region_3.0 | all-reduce | flops 4096 | bytes 32768 | tf_op jit(solution)/shard_map/psum | solution.py:38
  209.6 16.2 %psum.109 = f32[2,64,32]{1,2,0:T(8,128)S(1)} all-reduce(f32[2,64,32]{1,2,0:T(8,128)S(1)} %psum.108), channel_id=1, replica_groups=mesh['sy_0'=4,'sy_1'=4,'sx'=8,'wl'=2] {'sy_1'}, use_global_device_ids=true, to_apply=%region_4.0 | all-reduce | flops 4096 | bytes 32768 | tf_op jit(solution)/shard_map/psum | solution.py:38
  225.8 27.1 %psum.110 = f32[2,64,32]{1,2,0:T(8,128)S(1)} all-reduce(f32[2,64,32]{1,2,0:T(8,128)S(1)} %psum.109), channel_id=1, replica_groups=mesh['sy_0'=4,'sy_1'=4,'sx'=8,'wl'=2] {'sx'}, use_global_device_ids=true, to_apply=%region_5.0 | all-reduce | flops 4096 | bytes 32768 | tf_op jit(solution)/shard_map/psum | solution.py:38
  254.6 3.8 collective-permute-start.19
  258.4 2.1 collective-permute-start.14
  260.6 3.7 collective-permute-start.13
  266.2 3.3 collective-permute-start.18
  271.2 6.0 collective-permute-start.16
  279.2 5.6 collective-permute-done.15
  287.0 3.3 collective-permute-done.17
  296.7 6.8 %fusion.38 = f32[2,64,2,1536]{3,1,2,0:T(8,128)S(1)} fusion(bf16[2,1536,1536,1]{2,1,0,3:T(8,128)(2,1)} %bitcast.698, bf16[2,64,1536,1]{2,1,0,3:T(8,128)(2,1)S(1)} %reshape.2909), kind=kOutput, calls=%fused_computation.116 | convolution fusion | flops 1207959552 | bytes 11403264 | tf_op jit(solution)/shard_map/dot_general | solution.py:94
  307.0 16.2 %psum.111 = f32[2,64,32]{1,2,0:T(8,128)S(1)} all-reduce(f32[2,64,32]{1,2,0:T(8,128)S(1)} %pad_maximum_fusion.3), channel_id=1, replica_groups=mesh['sy_0'=4,'sy_1'=4,'sx'=8,'wl'=2] {'sy_0'}, use_global_device_ids=true, to_apply=%region_6.0 | all-reduce | flops 4096 | bytes 32768 | tf_op jit(solution)/shard_map/psum | solution.py:38
  323.1 14.5 %psum.112 = f32[2,64,32]{1,2,0:T(8,128)S(1)} all-reduce(f32[2,64,32]{1,2,0:T(8,128)S(1)} %psum.111), channel_id=1, replica_groups=mesh['sy_0'=4,'sy_1'=4,'sx'=8,'wl'=2] {'sy_1'}, use_global_device_ids=true, to_apply=%region_7.0 | all-reduce | flops 4096 | bytes 32768 | tf_op jit(solution)/shard_map/psum | solution.py:38
  337.6 27.6 %psum.113 = f32[2,64,32]{1,2,0:T(8,128)S(1)} all-reduce(f32[2,64,32]{1,2,0:T(8,128)S(1)} %psum.112), channel_id=1, replica_groups=mesh['sy_0'=4,'sy_1'=4,'sx'=8,'wl'=2] {'sx'}, use_global_device_ids=true, to_apply=%region_8.0 | all-reduce | flops 4096 | bytes 32768 | tf_op jit(solution)/shard_map/psum | solution.py:38
  369.1 3.8 collective-permute-start.22
  374.9 2.5 collective-permute-start.20
  377.5 5.0 collective-permute-start.26
  384.2 5.3 collective-permute-start.24
  391.5 5.6 collective-permute-done.23
  399.3 3.3 collective-permute-done.25
  408.8 6.8 fusion.36
  419.0 15.6 %psum.114 = f32[2,64,32]{1,2,0:T(8,128)S(1)} all-reduce(f32[2,64,32]{1,2,0:T(8,128)S(1)} %pad_maximum_fusion.4), channel_id=1, replica_groups=mesh['sy_0'=4,'sy_1'=4,'sx'=8,'wl'=2] {'sy_0'}, use_global_device_ids=true, to_apply=%region_9.0 | all-reduce | flops 4096 | bytes 32768 | tf_op jit(solution)/shard_map/psum | solution.py:38
  434.6 15.5 %psum.115 = f32[2,64,32]{1,2,0:T(8,128)S(1)} all-reduce(f32[2,64,32]{1,2,0:T(8,128)S(1)} %psum.114), channel_id=1, replica_groups=mesh['sy_0'=4,'sy_1'=4,'sx'=8,'wl'=2] {'sy_1'}, use_global_device_ids=true, to_apply=%region_10.0 | all-reduce | flops 4096 | bytes 32768 | tf_op jit(solution)/shard_map/psum | solution.py:38
  450.1 26.9 %psum.116 = f32[2,64,32]{1,2,0:T(8,128)S(1)} all-reduce(f32[2,64,32]{1,2,0:T(8,128)S(1)} %psum.115), channel_id=1, replica_groups=mesh['sy_0'=4,'sy_1'=4,'sx'=8,'wl'=2] {'sx'}, use_global_device_ids=true, to_apply=%region_11.0 | all-reduce | flops 4096 | bytes 32768 | tf_op jit(solution)/shard_map/psum | solution.py:38
  478.7 2.5 collective-permute-start.35
  481.3 3.3 collective-permute-start.30
  484.6 2.5 collective-permute-start.29
  489.1 4.5 collective-permute-start.34
  495.3 6.0 collective-permute-start.32
  503.3 5.6 collective-permute-done.31
  511.1 3.3 collective-permute-done.33
  520.6 6.8 %fusion.34 = f32[2,64,2,1536]{3,1,2,0:T(8,128)S(1)} fusion(bf16[2,1536,1536,1]{2,1,0,3:T(8,128)(2,1)} %bitcast.700, bf16[2,64,1536,1]{2,1,0,3:T(8,128)(2,1)S(1)} %reshape.2919), kind=kOutput, calls=%fused_computation.112 | convolution fusion | flops 1207959552 | bytes 11403264 | tf_op jit(solution)/shard_map/dot_general | solution.py:94
  530.8 14.7 %psum.117 = f32[2,64,32]{1,2,0:T(8,128)S(1)} all-reduce(f32[2,64,32]{1,2,0:T(8,128)S(1)} %pad_maximum_fusion.5), channel_id=1, replica_groups=mesh['sy_0'=4,'sy_1'=4,'sx'=8,'wl'=2] {'sy_0'}, use_global_device_ids=true, to_apply=%region_12.0 | all-reduce | flops 4096 | bytes 32768 | tf_op jit(solution)/shard_map/psum | solution.py:38
  545.4 16.1 %psum.118 = f32[2,64,32]{1,2,0:T(8,128)S(1)} all-reduce(f32[2,64,32]{1,2,0:T(8,128)S(1)} %psum.117), channel_id=1, replica_groups=mesh['sy_0'=4,'sy_1'=4,'sx'=8,'wl'=2] {'sy_1'}, use_global_device_ids=true, to_apply=%region_13.0 | all-reduce | flops 4096 | bytes 32768 | tf_op jit(solution)/shard_map/psum | solution.py:38
  561.5 26.9 %psum.119 = f32[2,64,32]{1,2,0:T(8,128)S(1)} all-reduce(f32[2,64,32]{1,2,0:T(8,128)S(1)} %psum.118), channel_id=1, replica_groups=mesh['sy_0'=4,'sy_1'=4,'sx'=8,'wl'=2] {'sx'}, use_global_device_ids=true, to_apply=%region_14.0 | all-reduce | flops 4096 | bytes 32768 | tf_op jit(solution)/shard_map/psum | solution.py:38
  590.1 2.7 collective-permute-start.43
  592.9 3.1 collective-permute-start.38
  596.0 2.7 collective-permute-start.37
  600.6 4.3 collective-permute-start.42
  607.3 6.0 collective-permute-start.40
  615.3 5.6 collective-permute-done.39
  623.1 3.3 collective-permute-done.41
  629.9 6.8 fusion.32
  639.5 2.8 collective-permute-start.46
  642.3 3.1 collective-permute-start.45
  647.3 5.1 collective-permute-start.50
  652.4 6.0 collective-permute-start.48
  660.5 5.6 collective-permute-done.47
  668.3 3.3 collective-permute-done.49
  (412 shorter events, 143.7 us)
Async XLA Ops:
  12.3 12.7 %copy-start.2 = (f32[1,1,2,32,4,384]{5,4,3,2,1,0:T(4,128)S(1)}, f32[1,1,2,32,4,384]{5,4,3,2,1,0:T(4,128)}, u32[]{:S(2)}) copy-start(f32[1,1,2,32,4,384]{5,4,3,2,1,0:T(4,128)} %param.120) | copy-start | bytes 1179652
  34.2 1.1 copy-start
  35.4 17.5 %copy-start.3 = (f32[1,1,2,32,4,384]{5,4,3,2,1,0:T(4,128)S(1)}, f32[1,1,2,32,4,384]{5,4,3,2,1,0:T(4,128)}, u32[]{:S(2)}) copy-start(f32[1,1,2,32,4,384]{5,4,3,2,1,0:T(4,128)} %param.119) | copy-start | bytes 1179652
  36.2 48.9 %collective-permute-start.7 = (f32[2,64,384]{2,1,0:T(8,128)}, f32[2,64,384]{2,1,0:T(8,128)S(1)}, u32[]{:S(2)}, u32[]{:S(2)}) collective-permute-start(f32[2,64,384]{2,1,0:T(8,128)} %get-tuple-element.741), channel_id=1, source_target_pairs={{2,0},{4,2},{6,4},{8,6},{10,8},{12,10},{14,12},{3,1},{5,3},{7,5},{... | collective-permute-start | bytes 589832 | tf_op jit(solution)/shard_map/ppermute | solution.py:21
  38.6 17.1 %collective-permute-start.2 = (f32[2,2,64]{2,1,0:T(2,128)S(1)}, f32[2,2,64]{2,1,0:T(2,128)S(1)}, u32[]{:S(2)}, u32[]{:S(2)}) collective-permute-start(f32[2,2,64]{2,1,0:T(2,128)S(1)} %pad_maximum_fusion.8), channel_id=1, source_target_pairs={{2,0},{4,2},{6,4},{8,6},{10,8},{12,10},{14,12},{3,1},{5,3},{7,5},{... | collective-permute-start | bytes 3080 | tf_op jit(solution)/shard_map/ppermute | solution.py:21
  40.6 19.6 %collective-permute-start.1 = (f32[2,2,64]{2,1,0:T(2,128)S(1)}, f32[2,2,64]{2,1,0:T(2,128)S(1)}, u32[]{:S(2)}, u32[]{:S(2)}) collective-permute-start(f32[2,2,64]{2,1,0:T(2,128)S(1)} %pad_maximum_fusion.7), channel_id=1, source_target_pairs={{0,2},{2,4},{4,6},{6,8},{8,10},{10,12},{12,14},{1,3},{3,5},{5,7},{... | collective-permute-start | bytes 3080 | tf_op jit(solution)/shard_map/ppermute | solution.py:21
  44.4 31.6 %collective-permute-start = (f32[2,64,384]{2,1,0:T(8,128)S(1)}, f32[2,64,384]{2,1,0:T(8,128)}, u32[]{:S(2)}, u32[]{:S(2)}) collective-permute-start(f32[2,64,384]{2,1,0:T(8,128)S(1)} %get-tuple-element.740), channel_id=1, source_target_pairs={{0,16},{16,32},{32,48},{48,64},{64,80},{80,96},{96,112},{112,128},... | collective-permute-start | bytes 589832 | tf_op jit(solution)/shard_map/ppermute | solution.py:21
  47.8 34.3 %collective-permute-start.6 = (f32[2,64,384]{2,1,0:T(8,128)}, f32[2,64,384]{2,1,0:T(8,128)}, u32[]{:S(2)}, u32[]{:S(2)}) collective-permute-start(f32[2,64,384]{2,1,0:T(8,128)} %get-tuple-element.743), channel_id=1, source_target_pairs={{0,2},{2,4},{4,6},{6,8},{8,10},{10,12},{12,14},{1,3},{3,5},{5,7},{... | collective-permute-start | bytes 589832 | tf_op jit(solution)/shard_map/ppermute | solution.py:21
  55.6 33.6 %collective-permute-start.4 = (f32[2,64,384]{2,1,0:T(8,128)}, f32[2,64,384]{2,1,0:T(8,128)}, u32[]{:S(2)}, u32[]{:S(2)}) collective-permute-start(f32[2,64,384]{2,1,0:T(8,128)} %get-tuple-element.742), channel_id=1, source_target_pairs={{16,0},{32,16},{48,32},{64,48},{80,64},{96,80},{112,96},{128,112},... | collective-permute-start | bytes 589832 | tf_op jit(solution)/shard_map/ppermute | solution.py:21
  60.2 7.6 %collective-permute-start.3 = (f32[2,2,64]{2,1,0:T(2,128)S(1)}, f32[2,2,64]{2,1,0:T(2,128)S(1)}, u32[]{:S(2)}, u32[]{:S(2)}) collective-permute-start(f32[2,2,64]{2,1,0:T(2,128)S(1)} %pad_maximum_fusion.9), channel_id=1, source_target_pairs={{0,16},{16,32},{32,48},{48,64},{64,80},{80,96},{96,112},{112,128},... | collective-permute-start | bytes 3080 | tf_op jit(solution)/shard_map/ppermute | solution.py:21
  67.8 5.5 collective-permute-start.5
  73.3 19.1 %collective-permute-start.8 = (f32[1,3,2,32,384]{4,3,2,1,0:T(8,128)}, f32[1,3,2,32,384]{4,3,2,1,0:T(8,128)S(1)}, u32[]{:S(2)}, u32[]{:S(2)}) collective-permute-start(f32[1,3,2,32,384]{4,3,2,1,0:T(8,128)} %maximum_bitcast_fusion.3), channel_id=1, source_target_pairs={{0,16},{16,32},{32,48},{48,64},{64,80},{80,96},{96,112},{112,128},... | collective-permute-start | bytes 884744 | tf_op jit(solution)/shard_map/ppermute | solution.py:31
  76.0 17.4 %collective-permute-start.9 = (f32[1,3,2,32,384]{4,3,2,1,0:T(8,128)}, f32[1,3,2,32,384]{4,3,2,1,0:T(8,128)S(1)}, u32[]{:S(2)}, u32[]{:S(2)}) collective-permute-start(f32[1,3,2,32,384]{4,3,2,1,0:T(8,128)} %maximum_bitcast_fusion.4), channel_id=1, source_target_pairs={{16,0},{32,16},{48,32},{64,48},{80,64},{96,80},{112,96},{128,112},... | collective-permute-start | bytes 884744 | tf_op jit(solution)/shard_map/ppermute | solution.py:32
  93.4 6.2 copy-start.5
  93.4 9.5 %copy-start.4 = (f32[2,64,1,1]{3,1,0,2:T(8,128)S(1)}, f32[2,64,1,1]{3,1,0,2:T(8,128)}, u32[]{:S(2)}) copy-start(f32[2,64,1,1]{3,1,0,2:T(8,128)} %get-tuple-element.804) | copy-start | bytes 1540
  94.5 12.2 %collective-permute-start.10 = (f32[5,1,2,32,384]{4,3,2,1,0:T(8,128)}, f32[5,1,2,32,384]{4,3,2,1,0:T(8,128)}, u32[]{:S(2)}, u32[]{:S(2)}) collective-permute-start(f32[5,1,2,32,384]{4,3,2,1,0:T(8,128)} %get-tuple-element.718), channel_id=1, source_target_pairs={{0,2},{2,4},{4,6},{6,8},{8,10},{10,12},{12,14},{1,3},{3,5},{5,7},{... | collective-permute-start | bytes 1474568 | tf_op jit(solution)/shard_map/ppermute | solution.py:31
  104.6 11.0 %collective-permute-start.11 = (f32[5,1,2,32,384]{4,3,2,1,0:T(8,128)}, f32[5,1,2,32,384]{4,3,2,1,0:T(8,128)}, u32[]{:S(2)}, u32[]{:S(2)}) collective-permute-start(f32[5,1,2,32,384]{4,3,2,1,0:T(8,128)} %get-tuple-element.719), channel_id=1, source_target_pairs={{2,0},{4,2},{6,4},{8,6},{10,8},{12,10},{14,12},{3,1},{5,3},{7,5},{... | collective-permute-start | bytes 1474568 | tf_op jit(solution)/shard_map/ppermute | solution.py:32
  119.2 60.7 %copy-start.1 = (f32[2,32,32]{2,1,0:T(8,128)S(1)}, f32[2,32,32]{2,1,0:T(8,128)}, u32[]{:S(2)}) copy-start(f32[2,32,32]{2,1,0:T(8,128)} %param.121) | copy-start | bytes 24580
  254.6 37.5 %collective-permute-start.19 = (f32[2,64,384]{2,1,0:T(8,128)}, f32[2,64,384]{2,1,0:T(8,128)S(1)}, u32[]{:S(2)}, u32[]{:S(2)}) collective-permute-start(f32[2,64,384]{2,1,0:T(8,128)} %get-tuple-element.737), channel_id=1, source_target_pairs={{2,0},{4,2},{6,4},{8,6},{10,8},{12,10},{14,12},{3,1},{5,3},{7,5},{... | collective-permute-start | bytes 589832 | tf_op jit(solution)/shard_map/ppermute | solution.py:21
  258.4 12.7 %collective-permute-start.14 = (f32[2,2,64]{2,1,0:T(2,128)S(1)}, f32[2,2,64]{2,1,0:T(2,128)S(1)}, u32[]{:S(2)}, u32[]{:S(2)}) collective-permute-start(f32[2,2,64]{2,1,0:T(2,128)S(1)} %pad_maximum_fusion.12), channel_id=1, source_target_pairs={{2,0},{4,2},{6,4},{8,6},{10,8},{12,10},{14,12},{3,1},{5,3},{7,5},{... | collective-permute-start | bytes 3080 | tf_op jit(solution)/shard_map/ppermute | solution.py:21
  260.6 16.7 %collective-permute-start.13 = (f32[2,2,64]{2,1,0:T(2,128)S(1)}, f32[2,2,64]{2,1,0:T(2,128)S(1)}, u32[]{:S(2)}, u32[]{:S(2)}) collective-permute-start(f32[2,2,64]{2,1,0:T(2,128)S(1)} %pad_maximum_fusion.11), channel_id=1, source_target_pairs={{0,2},{2,4},{4,6},{6,8},{8,10},{10,12},{12,14},{1,3},{3,5},{5,7},{... | collective-permute-start | bytes 3080 | tf_op jit(solution)/shard_map/ppermute | solution.py:21
  264.3 26.2 %collective-permute-start.12 = (f32[2,64,384]{2,1,0:T(8,128)}, f32[2,64,384]{2,1,0:T(8,128)S(1)}, u32[]{:S(2)}, u32[]{:S(2)}) collective-permute-start(f32[2,64,384]{2,1,0:T(8,128)} %get-tuple-element.736), channel_id=1, source_target_pairs={{0,16},{16,32},{32,48},{48,64},{64,80},{80,96},{96,112},{112,128},... | collective-permute-start | bytes 589832 | tf_op jit(solution)/shard_map/ppermute | solution.py:21
  266.2 24.3 %collective-permute-start.18 = (f32[2,64,384]{2,1,0:T(8,128)}, f32[2,64,384]{2,1,0:T(8,128)S(1)}, u32[]{:S(2)}, u32[]{:S(2)}) collective-permute-start(f32[2,64,384]{2,1,0:T(8,128)} %get-tuple-element.739), channel_id=1, source_target_pairs={{0,2},{2,4},{4,6},{6,8},{8,10},{10,12},{12,14},{1,3},{3,5},{5,7},{... | collective-permute-start | bytes 589832 | tf_op jit(solution)/shard_map/ppermute | solution.py:21
  271.2 23.2 %collective-permute-start.16 = (f32[2,64,384]{2,1,0:T(8,128)}, f32[2,64,384]{2,1,0:T(8,128)S(1)}, u32[]{:S(2)}, u32[]{:S(2)}) collective-permute-start(f32[2,64,384]{2,1,0:T(8,128)} %get-tuple-element.738), channel_id=1, source_target_pairs={{16,0},{32,16},{48,32},{64,48},{80,64},{96,80},{112,96},{128,112},... | collective-permute-start | bytes 589832 | tf_op jit(solution)/shard_map/ppermute | solution.py:21
  277.2 7.6 %collective-permute-start.15 = (f32[2,2,64]{2,1,0:T(2,128)S(1)}, f32[2,2,64]{2,1,0:T(2,128)S(1)}, u32[]{:S(2)}, u32[]{:S(2)}) collective-permute-start(f32[2,2,64]{2,1,0:T(2,128)S(1)} %pad_maximum_fusion.13), channel_id=1, source_target_pairs={{0,16},{16,32},{32,48},{48,64},{64,80},{80,96},{96,112},{112,128},... | collective-permute-start | bytes 3080 | tf_op jit(solution)/shard_map/ppermute | solution.py:21
  284.8 5.5 collective-permute-start.17
  367.0 37.5 %collective-permute-start.27 = (f32[2,64,384]{2,1,0:T(8,128)}, f32[2,64,384]{2,1,0:T(8,128)S(1)}, u32[]{:S(2)}, u32[]{:S(2)}) collective-permute-start(f32[2,64,384]{2,1,0:T(8,128)} %get-tuple-element.733), channel_id=1, source_target_pairs={{2,0},{4,2},{6,4},{8,6},{10,8},{12,10},{14,12},{3,1},{5,3},{7,5},{... | collective-permute-start | bytes 589832 | tf_op jit(solution)/shard_map/ppermute | solution.py:21
  369.1 15.1 %collective-permute-start.22 = (f32[2,2,64]{2,1,0:T(2,128)S(1)}, f32[2,2,64]{2,1,0:T(2,128)S(1)}, u32[]{:S(2)}, u32[]{:S(2)}) collective-permute-start(f32[2,2,64]{2,1,0:T(2,128)S(1)} %pad_maximum_fusion.16), channel_id=1, source_target_pairs={{2,0},{4,2},{6,4},{8,6},{10,8},{12,10},{14,12},{3,1},{5,3},{7,5},{... | collective-permute-start | bytes 3080 | tf_op jit(solution)/shard_map/ppermute | solution.py:21
  372.9 16.7 %collective-permute-start.21 = (f32[2,2,64]{2,1,0:T(2,128)S(1)}, f32[2,2,64]{2,1,0:T(2,128)S(1)}, u32[]{:S(2)}, u32[]{:S(2)}) collective-permute-start(f32[2,2,64]{2,1,0:T(2,128)S(1)} %pad_maximum_fusion.15), channel_id=1, source_target_pairs={{0,2},{2,4},{4,6},{6,8},{8,10},{10,12},{12,14},{1,3},{3,5},{5,7},{... | collective-permute-start | bytes 3080 | tf_op jit(solution)/shard_map/ppermute | solution.py:21
  374.9 27.9 %collective-permute-start.20 = (f32[2,64,384]{2,1,0:T(8,128)}, f32[2,64,384]{2,1,0:T(8,128)S(1)}, u32[]{:S(2)}, u32[]{:S(2)}) collective-permute-start(f32[2,64,384]{2,1,0:T(8,128)} %get-tuple-element.732), channel_id=1, source_target_pairs={{0,16},{16,32},{32,48},{48,64},{64,80},{80,96},{96,112},{112,128},... | collective-permute-start | bytes 589832 | tf_op jit(solution)/shard_map/ppermute | solution.py:21
  377.5 25.4 %collective-permute-start.26 = (f32[2,64,384]{2,1,0:T(8,128)}, f32[2,64,384]{2,1,0:T(8,128)S(1)}, u32[]{:S(2)}, u32[]{:S(2)}) collective-permute-start(f32[2,64,384]{2,1,0:T(8,128)} %get-tuple-element.735), channel_id=1, source_target_pairs={{0,2},{2,4},{4,6},{6,8},{8,10},{10,12},{12,14},{1,3},{3,5},{5,7},{... | collective-permute-start | bytes 589832 | tf_op jit(solution)/shard_map/ppermute | solution.py:21
  384.2 22.1 %collective-permute-start.24 = (f32[2,64,384]{2,1,0:T(8,128)}, f32[2,64,384]{2,1,0:T(8,128)S(1)}, u32[]{:S(2)}, u32[]{:S(2)}) collective-permute-start(f32[2,64,384]{2,1,0:T(8,128)} %get-tuple-element.734), channel_id=1, source_target_pairs={{16,0},{32,16},{48,32},{64,48},{80,64},{96,80},{112,96},{128,112},... | collective-permute-start | bytes 589832 | tf_op jit(solution)/shard_map/ppermute | solution.py:21
  389.6 7.6 %collective-permute-start.23 = (f32[2,2,64]{2,1,0:T(2,128)S(1)}, f32[2,2,64]{2,1,0:T(2,128)S(1)}, u32[]{:S(2)}, u32[]{:S(2)}) collective-permute-start(f32[2,2,64]{2,1,0:T(2,128)S(1)} %pad_maximum_fusion.17), channel_id=1, source_target_pairs={{0,16},{16,32},{32,48},{48,64},{64,80},{80,96},{96,112},{112,128},... | collective-permute-start | bytes 3080 | tf_op jit(solution)/shard_map/ppermute | solution.py:21
  397.2 5.5 collective-permute-start.25
  478.7 37.5 %collective-permute-start.35 = (f32[2,64,384]{2,1,0:T(8,128)}, f32[2,64,384]{2,1,0:T(8,128)S(1)}, u32[]{:S(2)}, u32[]{:S(2)}) collective-permute-start(f32[2,64,384]{2,1,0:T(8,128)} %get-tuple-element.729), channel_id=1, source_target_pairs={{2,0},{4,2},{6,4},{8,6},{10,8},{12,10},{14,12},{3,1},{5,3},{7,5},{... | collective-permute-start | bytes 589832 | tf_op jit(solution)/shard_map/ppermute | solution.py:21
  481.3 14.0 %collective-permute-start.30 = (f32[2,2,64]{2,1,0:T(2,128)S(1)}, f32[2,2,64]{2,1,0:T(2,128)S(1)}, u32[]{:S(2)}, u32[]{:S(2)}) collective-permute-start(f32[2,2,64]{2,1,0:T(2,128)S(1)} %pad_maximum_fusion.20), channel_id=1, source_target_pairs={{2,0},{4,2},{6,4},{8,6},{10,8},{12,10},{14,12},{3,1},{5,3},{7,5},{... | collective-permute-start | bytes 3080 | tf_op jit(solution)/shard_map/ppermute | solution.py:21
  484.6 16.7 %collective-permute-start.29 = (f32[2,2,64]{2,1,0:T(2,128)S(1)}, f32[2,2,64]{2,1,0:T(2,128)S(1)}, u32[]{:S(2)}, u32[]{:S(2)}) collective-permute-start(f32[2,2,64]{2,1,0:T(2,128)S(1)} %pad_maximum_fusion.19), channel_id=1, source_target_pairs={{0,2},{2,4},{4,6},{6,8},{8,10},{10,12},{12,14},{1,3},{3,5},{5,7},{... | collective-permute-start | bytes 3080 | tf_op jit(solution)/shard_map/ppermute | solution.py:21
  487.2 27.5 %collective-permute-start.28 = (f32[2,64,384]{2,1,0:T(8,128)}, f32[2,64,384]{2,1,0:T(8,128)S(1)}, u32[]{:S(2)}, u32[]{:S(2)}) collective-permute-start(f32[2,64,384]{2,1,0:T(8,128)} %get-tuple-element.728), channel_id=1, source_target_pairs={{0,16},{16,32},{32,48},{48,64},{64,80},{80,96},{96,112},{112,128},... | collective-permute-start | bytes 589832 | tf_op jit(solution)/shard_map/ppermute | solution.py:21
  489.1 25.6 %collective-permute-start.34 = (f32[2,64,384]{2,1,0:T(8,128)}, f32[2,64,384]{2,1,0:T(8,128)S(1)}, u32[]{:S(2)}, u32[]{:S(2)}) collective-permute-start(f32[2,64,384]{2,1,0:T(8,128)} %get-tuple-element.731), channel_id=1, source_target_pairs={{0,2},{2,4},{4,6},{6,8},{8,10},{10,12},{12,14},{1,3},{3,5},{5,7},{... | collective-permute-start | bytes 589832 | tf_op jit(solution)/shard_map/ppermute | solution.py:21
  495.3 22.8 %collective-permute-start.32 = (f32[2,64,384]{2,1,0:T(8,128)}, f32[2,64,384]{2,1,0:T(8,128)S(1)}, u32[]{:S(2)}, u32[]{:S(2)}) collective-permute-start(f32[2,64,384]{2,1,0:T(8,128)} %get-tuple-element.730), channel_id=1, source_target_pairs={{16,0},{32,16},{48,32},{64,48},{80,64},{96,80},{112,96},{128,112},... | collective-permute-start | bytes 589832 | tf_op jit(solution)/shard_map/ppermute | solution.py:21
  501.4 7.6 %collective-permute-start.31 = (f32[2,2,64]{2,1,0:T(2,128)S(1)}, f32[2,2,64]{2,1,0:T(2,128)S(1)}, u32[]{:S(2)}, u32[]{:S(2)}) collective-permute-start(f32[2,2,64]{2,1,0:T(2,128)S(1)} %pad_maximum_fusion.21), channel_id=1, source_target_pairs={{0,16},{16,32},{32,48},{48,64},{64,80},{80,96},{96,112},{112,128},... | collective-permute-start | bytes 3080 | tf_op jit(solution)/shard_map/ppermute | solution.py:21
  508.9 5.5 collective-permute-start.33
  590.1 36.7 %collective-permute-start.43 = (f32[2,64,384]{2,1,0:T(8,128)S(1)}, f32[2,64,384]{2,1,0:T(8,128)S(1)}, u32[]{:S(2)}, u32[]{:S(2)}) collective-permute-start(f32[2,64,384]{2,1,0:T(8,128)S(1)} %get-tuple-element.725), channel_id=1, source_target_pairs={{2,0},{4,2},{6,4},{8,6},{10,8},{12,10},{14,12},{3,1},{5,3},{7,5},{... | collective-permute-start | bytes 589832 | tf_op jit(solution)/shard_map/ppermute | solution.py:21
  592.9 14.4 %collective-permute-start.38 = (f32[2,2,64]{2,1,0:T(2,128)S(1)}, f32[2,2,64]{2,1,0:T(2,128)S(1)}, u32[]{:S(2)}, u32[]{:S(2)}) collective-permute-start(f32[2,2,64]{2,1,0:T(2,128)S(1)} %pad_maximum_fusion.24), channel_id=1, source_target_pairs={{2,0},{4,2},{6,4},{8,6},{10,8},{12,10},{14,12},{3,1},{5,3},{7,5},{... | collective-permute-start | bytes 3080 | tf_op jit(solution)/shard_map/ppermute | solution.py:21
  596.0 17.3 %collective-permute-start.37 = (f32[2,2,64]{2,1,0:T(2,128)S(1)}, f32[2,2,64]{2,1,0:T(2,128)S(1)}, u32[]{:S(2)}, u32[]{:S(2)}) collective-permute-start(f32[2,2,64]{2,1,0:T(2,128)S(1)} %pad_maximum_fusion.23), channel_id=1, source_target_pairs={{0,2},{2,4},{4,6},{6,8},{8,10},{10,12},{12,14},{1,3},{3,5},{5,7},{... | collective-permute-start | bytes 3080 | tf_op jit(solution)/shard_map/ppermute | solution.py:21
  598.7 27.9 %collective-permute-start.36 = (f32[2,64,384]{2,1,0:T(8,128)}, f32[2,64,384]{2,1,0:T(8,128)S(1)}, u32[]{:S(2)}, u32[]{:S(2)}) collective-permute-start(f32[2,64,384]{2,1,0:T(8,128)} %get-tuple-element.724), channel_id=1, source_target_pairs={{0,16},{16,32},{32,48},{48,64},{64,80},{80,96},{96,112},{112,128},... | collective-permute-start | bytes 589832 | tf_op jit(solution)/shard_map/ppermute | solution.py:21
  600.6 26.0 %collective-permute-start.42 = (f32[2,64,384]{2,1,0:T(8,128)}, f32[2,64,384]{2,1,0:T(8,128)S(1)}, u32[]{:S(2)}, u32[]{:S(2)}) collective-permute-start(f32[2,64,384]{2,1,0:T(8,128)} %get-tuple-element.727), channel_id=1, source_target_pairs={{0,2},{2,4},{4,6},{6,8},{8,10},{10,12},{12,14},{1,3},{3,5},{5,7},{... | collective-permute-start | bytes 589832 | tf_op jit(solution)/shard_map/ppermute | solution.py:21
  607.3 20.0 %collective-permute-start.40 = (f32[2,64,384]{2,1,0:T(8,128)S(1)}, f32[2,64,384]{2,1,0:T(8,128)S(1)}, u32[]{:S(2)}, u32[]{:S(2)}) collective-permute-start(f32[2,64,384]{2,1,0:T(8,128)S(1)} %get-tuple-element.726), channel_id=1, source_target_pairs={{16,0},{32,16},{48,32},{64,48},{80,64},{96,80},{112,96},{128,112},... | collective-permute-start | bytes 589832 | tf_op jit(solution)/shard_map/ppermute | solution.py:21
  613.3 7.6 %collective-permute-start.39 = (f32[2,2,64]{2,1,0:T(2,128)S(1)}, f32[2,2,64]{2,1,0:T(2,128)S(1)}, u32[]{:S(2)}, u32[]{:S(2)}) collective-permute-start(f32[2,2,64]{2,1,0:T(2,128)S(1)} %pad_maximum_fusion.25), channel_id=1, source_target_pairs={{0,16},{16,32},{32,48},{48,64},{64,80},{80,96},{96,112},{112,128},... | collective-permute-start | bytes 3080 | tf_op jit(solution)/shard_map/ppermute | solution.py:21
  620.9 5.5 collective-permute-start.41
  637.5 34.5 %collective-permute-start.51 = (f32[2,64,384]{2,1,0:T(8,128)S(1)}, f32[2,64,384]{2,1,0:T(8,128)S(1)}, u32[]{:S(2)}, u32[]{:S(2)}) collective-permute-start(f32[2,64,384]{2,1,0:T(8,128)S(1)} %get-tuple-element.722), channel_id=1, source_target_pairs={{2,0},{4,2},{6,4},{8,6},{10,8},{12,10},{14,12},{3,1},{5,3},{7,5},{... | collective-permute-start | bytes 589832 | tf_op jit(solution)/shard_map/ppermute | solution.py:21
  639.5 12.9 %collective-permute-start.46 = (f32[2,2,64]{2,1,0:T(2,128)S(1)}, f32[2,2,64]{2,1,0:T(2,128)S(1)}, u32[]{:S(2)}, u32[]{:S(2)}) collective-permute-start(f32[2,2,64]{2,1,0:T(2,128)S(1)} %pad_maximum_fusion.28), channel_id=1, source_target_pairs={{2,0},{4,2},{6,4},{8,6},{10,8},{12,10},{14,12},{3,1},{5,3},{7,5},{... | collective-permute-start | bytes 3080 | tf_op jit(solution)/shard_map/ppermute | solution.py:21
  642.3 16.2 %collective-permute-start.45 = (f32[2,2,64]{2,1,0:T(2,128)S(1)}, f32[2,2,64]{2,1,0:T(2,128)S(1)}, u32[]{:S(2)}, u32[]{:S(2)}) collective-permute-start(f32[2,2,64]{2,1,0:T(2,128)S(1)} %pad_maximum_fusion.27), channel_id=1, source_target_pairs={{0,2},{2,4},{4,6},{6,8},{8,10},{10,12},{12,14},{1,3},{3,5},{5,7},{... | collective-permute-start | bytes 3080 | tf_op jit(solution)/shard_map/ppermute | solution.py:21
  645.4 26.5 %collective-permute-start.44 = (f32[2,64,384]{2,1,0:T(8,128)S(1)}, f32[2,64,384]{2,1,0:T(8,128)S(1)}, u32[]{:S(2)}, u32[]{:S(2)}) collective-permute-start(f32[2,64,384]{2,1,0:T(8,128)S(1)} %get-tuple-element.720), channel_id=1, source_target_pairs={{0,16},{16,32},{32,48},{48,64},{64,80},{80,96},{96,112},{112,128},... | collective-permute-start | bytes 589832 | tf_op jit(solution)/shard_map/ppermute | solution.py:21
  647.3 24.5 %collective-permute-start.50 = (f32[2,64,384]{2,1,0:T(8,128)S(1)}, f32[2,64,384]{2,1,0:T(8,128)S(1)}, u32[]{:S(2)}, u32[]{:S(2)}) collective-permute-start(f32[2,64,384]{2,1,0:T(8,128)S(1)} %get-tuple-element.723), channel_id=1, source_target_pairs={{0,2},{2,4},{4,6},{6,8},{8,10},{10,12},{12,14},{1,3},{3,5},{5,7},{... | collective-permute-start | bytes 589832 | tf_op jit(solution)/shard_map/ppermute | solution.py:21
  652.4 20.1 %collective-permute-start.48 = (f32[2,64,384]{2,1,0:T(8,128)S(1)}, f32[2,64,384]{2,1,0:T(8,128)S(1)}, u32[]{:S(2)}, u32[]{:S(2)}) collective-permute-start(f32[2,64,384]{2,1,0:T(8,128)S(1)} %get-tuple-element.721), channel_id=1, source_target_pairs={{16,0},{32,16},{48,32},{64,48},{80,64},{96,80},{112,96},{128,112},... | collective-permute-start | bytes 589832 | tf_op jit(solution)/shard_map/ppermute | solution.py:21
  658.5 7.6 %collective-permute-start.47 = (f32[2,2,64]{2,1,0:T(2,128)S(1)}, f32[2,2,64]{2,1,0:T(2,128)S(1)}, u32[]{:S(2)}, u32[]{:S(2)}) collective-permute-start(f32[2,2,64]{2,1,0:T(2,128)S(1)} %pad_maximum_fusion.29), channel_id=1, source_target_pairs={{0,16},{16,32},{32,48},{48,64},{64,80},{80,96},{96,112},{112,128},... | collective-permute-start | bytes 3080 | tf_op jit(solution)/shard_map/ppermute | solution.py:21
  666.1 5.5 collective-permute-start.49
where the time goes:
time: 687 us; the launch traced here: 676 us
  blocking collectives  290 us (42%)
  starting transfers between devices  162 us (24%)
  local copies, waits for them, and re-layouts  71.8 us (10%)
  matrix products  67.9 us (10%)
  waiting for transfers between devices  59.8 us (9%)
  other arithmetic  20.3 us (3%)
    psum x15, blocking collectives, over_axes(): return functools.reduce(lax.psum, axes, value)  290 us
    ppermute x48, starting transfers between devices, shifted(): return lax.ppermute(value, axis, pairs)  148 us
    ppermute x48, waiting for transfers between devices, shifted(): return lax.ppermute(value, axis, pairs)  52.7 us
    dot_general x6, matrix products, outgoing_traces(): jnp.dot(row_block, map_table, preferred_element_type=jnp.float32)  40.6 us
  transfers between devices with their start and end apart: 52, of which 13 were waited for; matrix products, arithmetic and copies ran while one was open for 7% of the time, Pallas kernels for 0%

commit v1 on v0

v1 whole, which is shorter than its diff:
```python
import functools

import jax
import jax.numpy as jnp
from jax import lax
from jax.experimental import pallas as pl
from jax.experimental.pallas import tpu as pltpu
from jax.sharding import PartitionSpec as P

ITERS = 6
LANES = 128
MESH = pl.DeviceIdType.MESH
HIGH = lax.Precision.HIGHEST
NORTH, SOUTH, WEST, EAST = 0, 1, 2, 3
OUT_OF = {NORTH: SOUTH, SOUTH: NORTH, WEST: EAST, EAST: WEST}


def dot(a, b, contract, precision=None):
    return lax.dot_general(
        a, b, (contract, ((), ())), preferred_element_type=jnp.float32, precision=precision
    )


def turned(pair, half):
    return jnp.concatenate([-pair[:, half:], pair[:, :half]], axis=1)


def kernel(
    dims,
    map_hbm,
    src_ref,
    res_ref,
    pro_ref,
    inv_ref,
    out_ref,
    coef_ref,
    table,
    lhs,
    low,
    sent,
    got,
    lift,
    res_split,
    corner_out,
    corner_in,
    part,
    plane_in,
    line_out,
    line_in,
    col_out,
    col_in,
    fix,
    map_sem,
    send_sem,
    recv_sem,
    csend_sem,
    crecv_sem,
    asend_sem,
    arecv_sem,
):
    ny, nx, nz, s2, q2, thirds = dims
    cells = thirds * LANES
    nsy = ny * nx
    rows_all = s2 + q2
    half_s, half_q = s2 // 2, q2 // 2
    sy, sx = lax.axis_index("sy"), lax.axis_index("sx")
    wl = lax.axis_index("wl")
    yy = sy // nx

    def dev(row, col):
        return (row, col, wl)

    up, down = lax.rem(sy + nsy - 1, nsy), lax.rem(sy + 1, nsy)
    left, right = lax.rem(sx + nz - 1, nz), lax.rem(sx + 1, nz)
    peer = {NORTH: dev(up, sx), SOUTH: dev(down, sx), WEST: dev(sy, left), EAST: dev(sy, right)}
    diag = (dev(up, left), dev(up, right), dev(down, left), dev(down, right))
    has = {NORTH: sy > 0, SOUTH: sy < nsy - 1, WEST: sx > 0, EAST: sx < nz - 1}
    has_diag = (
        (sy > 0) & (sx > 0),
        (sy > 0) & (sx < nz - 1),
        (sy < nsy - 1) & (sx > 0),
        (sy < nsy - 1) & (sx < nz - 1),
    )

    loads = [
        [pltpu.make_async_copy(map_hbm.at[t, h], table.at[t, h], map_sem.at[t, h]) for h in (0, 1)]
        for t in range(thirds)
    ]
    order = (0, *range(2, thirds), 1)
    for t in order:
        for h in (0, 1):
            loads[t][h].start()

    barrier = pltpu.get_barrier_semaphore()
    met = 0
    for target in (*peer.values(), *diag):
        pl.semaphore_signal(barrier, inc=1, device_id=target, device_id_type=MESH)
        met += 1
    for d in range(1, nsy):
        target = dev(lax.rem(sy + d, nsy), sx)
        pl.semaphore_signal(barrier, inc=1, device_id=target, device_id_type=MESH)
        met += 1
    for d in range(1, nz):
        target = dev(sy, lax.rem(sx + d, nz))
        pl.semaphore_signal(barrier, inc=1, device_id=target, device_id_type=MESH)
        met += 1
    pl.semaphore_wait(barrier, met)

    lane = lax.broadcasted_iota(jnp.int32, (1, LANES), 1)

    def rows_of(e):
        return rows_all if e in (2, 3) else s2

    def side_copy(e, side, t):
        par, rows = e % 2, rows_of(e)
        src = src_ref.at[side, t] if e == 1 else sent.at[side, t, pl.ds(0, rows)]
        return pltpu.make_async_remote_copy(
            src_ref=src,
            dst_ref=got.at[par, OUT_OF[side], t, pl.ds(0, rows)],
            send_sem=send_sem.at[side, t],
            recv_sem=recv_sem.at[par, OUT_OF[side], t],
            device_id=peer[side],
            device_id_type=MESH,
        )

    def corner_copy(e, k):
        par = e % 2
        return pltpu.make_async_remote_copy(
            src_ref=corner_out.at[par],
            dst_ref=corner_in.at[par, 3 - k],
            send_sem=csend_sem.at[par, k],
            recv_sem=crecv_sem.at[par, 3 - k],
            device_id=diag[k],
            device_id_type=MESH,
        )

    def send_corners(e, block):
        last = thirds - 1
        n0, n1 = block(NORTH, 0)[:, 0:1], block(NORTH, last)[:, LANES - 1 :]
        s0, s1 = block(SOUTH, 0)[:, 0:1], block(SOUTH, last)[:, LANES - 1 :]
        w0, w1 = block(WEST, 0)[:, 0:1], block(WEST, last)[:, LANES - 1 :]
        e0, e1 = block(EAST, 0)[:, 0:1], block(EAST, last)[:, LANES - 1 :]
        nw, ne, sw, se = n0 + w0, n1 + e0, s0 + w1, s1 + e1
        z = jnp.where(
            lane == 0, nw, jnp.where(lane == 1, ne, jnp.where(lane == 2, sw, se))
        )
        first = z[0:LANES].T[0:4]
        if z.shape[0] > s2:
            spare = jnp.zeros((2 * LANES - z.shape[0], LANES), jnp.float32)
            second = jnp.concatenate([z[LANES:], spare], axis=0).T[0:4]
        else:
            second = jnp.zeros_like(first)
        corner_out[e % 2] = jnp.concatenate([first, second], axis=0)
        for k in range(4):
            corner_copy(e, k).start()

    chunk = part.shape[2]

    def stage_a(a, j):
        d = j
        target = lax.rem(sy + d, nsy)
        return pltpu.make_async_remote_copy(
            src_ref=part.at[a, target // nx],
            dst_ref=plane_in.at[a, nsy - d],
            send_sem=asend_sem.at[a, 0],
            recv_sem=arecv_sem.at[a, 0],
            device_id=dev(target, sx),
            device_id_type=MESH,
        )

    def stage_b(a, d):
        return pltpu.make_async_remote_copy(
            src_ref=line_out.at[a],
            dst_ref=line_in.at[a, nz - d],
            send_sem=asend_sem.at[a, 1],
            recv_sem=arecv_sem.at[a, 1],
            device_id=dev(sy, lax.rem(sx + d, nz)),
            device_id_type=MESH,
        )

    def stage_c(a, d):
        return pltpu.make_async_remote_copy(
            src_ref=col_out.at[a],
            dst_ref=col_in.at[a, ny - d],
            send_sem=asend_sem.at[a, 2],
            recv_sem=arecv_sem.at[a, 2],
            device_id=dev(lax.rem(sy + d * nx, nsy), sx),
            device_id_type=MESH,
        )

    def whole(a, stage):
        buf = (plane_in, line_in, col_in)[stage]
        n = (nsy, nz, ny)[stage]
        ref = buf.at[a, pl.ds(1, n - 1)]
        return pltpu.make_async_remote_copy(
            src_ref=ref,
            dst_ref=ref,
            send_sem=asend_sem.at[a, stage],
            recv_sem=arecv_sem.at[a, stage],
            device_id=peer[EAST],
            device_id_type=MESH,
        )

    def summed(values):
        while len(values) > 1:
            values = [
                values[i] + values[i + 1] if i + 1 < len(values) else values[i]
                for i in range(0, len(values), 2)
            ]
        return values[0]

    def start_sum(a, payload):
        for j in range(ny):
            part[a, j] = payload[j * chunk : (j + 1) * chunk]
        for d in range(1, nsy):
            stage_a(a, d).start()

    def sum_b(a):
        whole(a, 0).wait_recv()
        plane_in[a, 0] = part[a, yy]
        line_out[a] = summed([plane_in[a, lax.rem(j - sy + nsy, nsy)] for j in range(nsy)])
        for d in range(1, nz):
            stage_b(a, d).start()

    def sum_c(a):
        whole(a, 1).wait_recv()
        line_in[a, 0] = line_out[a]
        col_out[a] = summed([line_in[a, lax.rem(j - sx + nz, nz)] for j in range(nz)])
        for d in range(1, ny):
            stage_c(a, d).start()

    def sum_end(a):
        whole(a, 2).wait_recv()
        col_in[a, 0] = col_out[a]
        return jnp.concatenate([col_in[a, lax.rem(j - yy + ny, ny)] for j in range(ny)], axis=0)

    for t in order:
        for side in range(4):
            side_copy(1, side, t).start()
    send_corners(1, lambda side, t: src_ref[side, t])

    res = res_ref[...]
    res_hi = res.astype(jnp.bfloat16)
    res_split[0:q2] = res_hi
    res_split[q2:] = (res - res_hi.astype(jnp.float32)).astype(jnp.bfloat16)
    lhs[s2:rows_all] = pro_ref[...].astype(jnp.bfloat16)

    def restrict(first, last):
        hi, lo = lhs[first:last], low[first:last]
        half = (last - first) // 2
        both = dot(res_split[...], hi, ((1,), (1,)))
        rest = dot(res_split[0:q2], lo, ((1,), (1,)))
        u = both[0:q2] + both[q2:] + rest
        return u[0:half_q] + turned(u[half_q:], half)

    def coarse(total):
        stacked = jnp.concatenate([total, turned(total, half_s)], axis=0)
        coef = dot(inv_ref[...], stacked, ((0,), (0,)), HIGH)
        return coef

    def stack_of(coef):
        return jnp.concatenate([coef, turned(coef, half_s)], axis=0)

    def lifted(coef, k):
        fix[...] = dot(stack_of(coef), lift[k], ((0,), (0,)), HIGH)

    def receive(e, fixed):
        par, rows = e % 2, rows_of(e)
        for k in range(4):
            corner_copy(e, k).wait_recv()
        tile = []
        for base in (0, 4) if rows > s2 else (0,):
            for k in range(4):
                row = corner_in[par, k, base + 3 - k : base + 4 - k]
                tile.append(jnp.where(has_diag[k], 0.5 * row, 0.0))
        spare = jnp.zeros((LANES - len(tile), LANES), jnp.float32)
        flat = jnp.concatenate([*tile, spare], axis=0).T
        cols = flat[:, 0:4]
        if rows > s2:
            cols = jnp.concatenate([cols, flat[0:q2, 4:8]], axis=0)
        nw, ne, sw, se = (cols[:, k : k + 1] for k in range(4))
        ends = {NORTH: (nw, ne), SOUTH: (sw, se), WEST: (nw, sw), EAST: (ne, se)}

        def incoming(side, t, first, last):
            value = jnp.where(has[side], got[par, side, t, first:last], 0.0)
            if t == 0:
                value += jnp.where(lane == 0, ends[side][0][first:last], 0.0)
            if t == thirds - 1:
                value += jnp.where(lane == LANES - 1, ends[side][1][first:last], 0.0)
            return value

        for t in order:
            for side in range(4):
                side_copy(e, OUT_OF[side], t).wait_recv()
                if rows > s2:
                    at = side * cells + t * LANES
                    extra = incoming(side, t, s2, rows)
                    hi = extra.astype(jnp.bfloat16)
                    lift[e - 2, :, at : at + LANES] = extra
                    lhs[s2:, at : at + LANES] = hi
                    low[s2:, at : at + LANES] = (extra - hi.astype(jnp.float32)).astype(jnp.bfloat16)
        if fixed is not None:
            lifted(fixed, 1)
        for t in order:
            for side in range(4):
                at = side * cells + t * LANES
                top = incoming(side, t, 0, s2)
                if fixed is not None:
                    top += fix[:, at : at + LANES]
                if e == ITERS:
                    out_ref[:, at : at + LANES] = top
                    continue
                hi = top.astype(jnp.bfloat16)
                lhs[0:s2, at : at + LANES] = hi
                low[0:s2, at : at + LANES] = (top - hi.astype(jnp.float32)).astype(jnp.bfloat16)
        for t in order:
            for side in range(4):
                side_copy(e, side, t).wait_send()
        for k in range(4):
            corner_copy(e, k).wait_send()

    def multiply(e):
        rows = rows_of(e)

        for t in (*order, None):
            if t == order[-1]:
                send_corners(e, lambda side, t: sent[side, t, 0:rows])
            if t is None:
                break
            for h in (0, 1):
                if e == 2:
                    loads[t][h].wait()
                product = dot(lhs[0:rows], table[t, h], ((1,), (0,)))
                for k in (0, 1):
                    side = 2 * h + k
                    re = product[:, 2 * k * LANES : (2 * k + 1) * LANES]
                    im = product[:, (2 * k + 1) * LANES : (2 * k + 2) * LANES]
                    a, b = half_s, s2
                    sent[side, t, 0:a] = re[0:a] - im[a:b] + src_ref[side, t, 0:a]
                    sent[side, t, a:b] = im[0:a] + re[a:b] + src_ref[side, t, a:b]
                    if rows > s2:
                        a, b = s2 + half_q, s2 + q2
                        sent[side, t, s2:a] = re[s2:a] - im[a:b]
                        sent[side, t, a:b] = im[s2:a] + re[a:b]
                    side_copy(e, side, t).start()

    coef = {}
    for i in range(1, ITERS + 1):
        if i == 3:
            sum_c(1)
            coef[1] = coarse(sum_end(1))
        elif i > 3:
            finish(i - 2)
        receive(i, coef.get(i - 2))
        if i == ITERS:
            break
        start_sum(i, restrict(0, s2))
        if i == 2:
            half = restrict(s2, rows_all)
            start_sum(0, jnp.concatenate([half, jnp.zeros((half_q, LANES - q2), jnp.float32)], axis=1))
        multiply(i + 1)
        sum_b(i)
        if i == 2:
            sum_b(0)
            sum_c(0)
            share = sum_end(0)[:, 0:q2]

            def finish(j):
                sum_c(j)
                total = sum_end(j) + dot(share, stack_of(coef[j - 1]), ((1,), (0,)), HIGH)
                coef[j] = coarse(total)

    finish(ITERS - 1)
    lifted(coef[ITERS - 1], 0)
    for side in range(4):
        for t in range(thirds):
            at = side * cells + t * LANES
            out_ref[:, at : at + LANES] += fix[:, at : at + LANES]
    coef_ref[...] = coef[ITERS - 1]
    for a in range(ITERS):
        for stage in range(3):
            whole(a, stage).wait_send()


def solution(mesh):
    nsy, nz = mesh.shape["sy"], mesh.shape["sx"]
    nx = 4
    ny = nsy // nx

    def per_device(interface_map, source_trace, restriction, prolongation, coarse_inverse):
        src_count, cells = source_trace.shape[3], source_trace.shape[5]
        width = restriction.shape[3]
        thirds = cells // LANES
        s2, q2 = 2 * src_count, 2 * width
        rows = s2 + q2
        depth = 4 * cells
        dims = (ny, nx, nz, s2, q2, thirds)
        table = interface_map.reshape(depth, 2, 2, 2, thirds, LANES)
        table = table.transpose(4, 2, 0, 3, 1, 5).reshape(thirds, 2, depth, 4 * LANES)
        sources = source_trace.reshape(s2, 4, thirds, LANES).transpose(1, 2, 0, 3)
        chunk = width // ny
        vmem = pl.BlockSpec(memory_space=pltpu.VMEM)
        traces, coef = pl.pallas_call(
            functools.partial(kernel, dims),
            out_shape=(
                jax.ShapeDtypeStruct((s2, depth), jnp.float32),
                jax.ShapeDtypeStruct((width, s2), jnp.float32),
            ),
            in_specs=[pl.BlockSpec(memory_space=pl.ANY), vmem, vmem, vmem, vmem],
            out_specs=(vmem, vmem),
            scratch_shapes=[
                pltpu.VMEM((thirds, 2, depth, 4 * LANES), jnp.bfloat16),
                pltpu.VMEM((rows, depth), jnp.bfloat16),
                pltpu.VMEM((rows, depth), jnp.bfloat16),
                pltpu.VMEM((4, thirds, rows, LANES), jnp.float32),
                pltpu.VMEM((2, 4, thirds, rows, LANES), jnp.float32),
                pltpu.VMEM((2, q2, depth), jnp.float32),
                pltpu.VMEM((2 * q2, depth), jnp.bfloat16),
                pltpu.VMEM((2, 8, LANES), jnp.float32),
                pltpu.VMEM((2, 4, 8, LANES), jnp.float32),
                pltpu.VMEM((ITERS, ny, chunk, LANES), jnp.float32),
                pltpu.VMEM((ITERS, nsy, chunk, LANES), jnp.float32),
                pltpu.VMEM((ITERS, chunk, LANES), jnp.float32),
                pltpu.VMEM((ITERS, nz, chunk, LANES), jnp.float32),
                pltpu.VMEM((ITERS, chunk, LANES), jnp.float32),
                pltpu.VMEM((ITERS, ny, chunk, LANES), jnp.float32),
                pltpu.VMEM((s2, depth), jnp.float32),
                pltpu.SemaphoreType.DMA((thirds, 2)),
                pltpu.SemaphoreType.DMA((4, thirds)),
                pltpu.SemaphoreType.DMA((2, 4, thirds)),
                pltpu.SemaphoreType.DMA((2, 4)),
                pltpu.SemaphoreType.DMA((2, 4)),
                pltpu.SemaphoreType.DMA((ITERS, 3)),
                pltpu.SemaphoreType.DMA((ITERS, 3)),
            ],
            compiler_params=pltpu.CompilerParams(
                collective_id=0, has_side_effects=True, vmem_limit_bytes=60 * 1024 * 1024
            ),
        )(
            table,
            sources,
            restriction.reshape(q2, depth),
            prolongation.reshape(q2, depth),
            coarse_inverse.reshape(q2, width),
        )
        coef = coef.reshape(width, 2, src_count).transpose(1, 2, 0)
        return traces.reshape(source_trace.shape), coef

    where = P(("wl", "sy"), "sx", None, None, None, None)
    return jax.shard_map(
        per_device,
        mesh=mesh,
        in_specs=(P(("wl", "sy"), "sx", None, None, None), where, where, where, P("wl", None, None)),
        out_specs=(where, P("wl", None, None)),
        check_vma=False,
    )
```

time: 687 us -> 164 us (0.24)
  the two profiles are of different devices: /device:TPU:80 before, /device:TPU:32 now
where the time goes in v1:
time: 164 us; the launch traced here: 162 us
  Pallas kernels  92.5 us (56%)
  local copies, waits for them, and re-layouts  68.9 us (42%)
    pallas_call x1, Pallas kernels, per_device(): pl.pallas_call(functools.partial(kernel, dims), out_shape=(jax.ShapeDtype...  92.5 us
    unnamed x9, local copies, waits for them, and re-layouts  25.3 us
    transpose x1, local copies, waits for them, and re-layouts, per_device(): table.transpose(4, 2, 0, 3, 1, 5).reshape(thirds, 2, depth, 4 * LANES)  23.7 us
    reshape x1, local copies, waits for them, and re-layouts, per_device(): table.transpose(4, 2, 0, 3, 1, 5).reshape(thirds, 2, depth, 4 * LANES)  14.7 us

profile of v1, /device:TPU:32, one launch (start us, length us, event | category | flops | bytes accessed | tf_op | source)
XLA Modules:
  0.0 162.1 jit_solution(9736344825492023355)
XLA Ops:
  0.6 23.7 %copy.9 = bf16[1,1,1536,2,1536]{2,4,3,1,0:T(8,128)(2,1)} copy(bf16[1,1,1536,2,1536]{4,3,2,1,0:T(2,128)(2,1)} %param.5) | data formatting | bytes 18874368 | tf_op args[0]
  24.3 23.7 %copy.10 = bf16[3,2,1536,2,2,128]{5,4,3,2,1,0:T(2,128)(2,1)} copy(bf16[3,2,1536,2,2,128]{2,5,0,3,1,4:T(8,128)(2,1)} %bitcast.16) | data formatting | bytes 18874368 | tf_op jit(solution)/shard_map/transpose | solution.py:399
  48.0 0.0 copy-start
  48.0 0.0 copy-start.1
  48.0 0.0 copy-start.2
  48.0 14.7 %reshape.29.map_hbm = bf16[3,2,1536,512]{3,2,1,0:T(8,128)(2,1)} reshape(bf16[3,2,1536,2,2,128]{5,4,3,2,1,0:T(2,128)(2,1)} %copy.10) | data formatting | bytes 18874368 | tf_op jit(solution)/shard_map/reshape | solution.py:399
  62.7 0.0 copy-done
  62.7 0.5 reshape.36
  63.2 1.1 copy.20
  64.3 0.0 copy-done.1
  64.3 0.8 copy.17
  65.1 0.0 copy-done.2
  65.1 0.8 copy.16
  65.9 92.5 %shard_map.68 = (f32[128,1536]{1,0:T(8,128)}, f32[32,128]{1,0:T(8,128)}) custom-call(bf16[3,2,1536,512]{3,2,1,0:T(8,128)(2,1)} %reshape.29.map_hbm, f32[4,3,128,128]{3,2,1,0:T(8,128)} %bitcast.17, f32[64,1536]{1,0:T(8,128)} %bitcast.19, f32[64,1536]{1,0:T(8,128)} %bitcast.18, f32[64,32]{1,0:T(8,128)} %bitcast.22), custom_call_target="tpu_custom_call" | custom-call | tf_op jit(solution)/shard_map/pallas_call | solution.py:403
  158.4 2.3 %reshape.34 = f32[1,1,2,64,4,384]{5,4,3,2,1,0:T(4,128)} reshape(f32[128,1536]{1,0:T(8,128)} %get-tuple-element.4) | data formatting | bytes 1572864 | tf_op jit(solution)/shard_map/reshape | solution.py:447
  160.7 0.8 reshape.35
  161.5 0.6 copy.21
Async XLA Ops:
  48.0 14.7 %copy-start = (f32[1,1,2,64,4,384]{5,4,3,2,1,0:T(4,128)S(1)}, f32[1,1,2,64,4,384]{5,4,3,2,1,0:T(4,128)}, u32[]{:S(2)}) copy-start(f32[1,1,2,64,4,384]{5,4,3,2,1,0:T(4,128)} %param.6) | copy-start | bytes 2359300
  48.0 16.4 %copy-start.1 = (f32[1,1,2,32,4,384]{5,4,3,2,1,0:T(4,128)S(1)}, f32[1,1,2,32,4,384]{5,4,3,2,1,0:T(4,128)}, u32[]{:S(2)}) copy-start(f32[1,1,2,32,4,384]{5,4,3,2,1,0:T(4,128)} %param.8) | copy-start | bytes 1179652
  48.0 17.1 %copy-start.2 = (f32[1,1,2,32,4,384]{5,4,3,2,1,0:T(4,128)S(1)}, f32[1,1,2,32,4,384]{5,4,3,2,1,0:T(4,128)}, u32[]{:S(2)}) copy-start(f32[1,1,2,32,4,384]{5,4,3,2,1,0:T(4,128)} %param.7) | copy-start | bytes 1179652

commit v2 on v1

--- a/solution.py
+++ b/solution.py
@@ -28,12 +28,17 @@
 def kernel(
     dims,
     map_hbm,
+    src_hbm,
+    res_hbm,
+    pro_hbm,
+    inv_ref,
+    out_hbm,
+    coef_ref,
+    raw,
+    src_raw,
+    res_raw,
+    pro_raw,
     src_ref,
-    res_ref,
-    pro_ref,
-    inv_ref,
-    out_ref,
-    coef_ref,
     table,
     lhs,
     low,
@@ -50,7 +55,9 @@
     col_out,
     col_in,
     fix,
+    last_sum,
     map_sem,
+    load_sem,
     send_sem,
     recv_sem,
     csend_sem,
@@ -82,14 +89,37 @@
         (sy < nsy - 1) & (sx < nz - 1),
     )
 
+    depth = 4 * cells
+    order = (0, *range(2, thirds), 1)
+    blocks = depth // LANES
+    flat_map = map_hbm.reshape(2 * depth, depth)
     loads = [
-        [pltpu.make_async_copy(map_hbm.at[t, h], table.at[t, h], map_sem.at[t, h]) for h in (0, 1)]
-        for t in range(thirds)
+        pltpu.make_async_copy(
+            flat_map.at[pl.ds(2 * LANES * b, 2 * LANES)],
+            raw.at[pl.ds(2 * LANES * b, 2 * LANES)],
+            map_sem.at[b],
+        )
+        for b in range(blocks)
     ]
-    order = (0, *range(2, thirds), 1)
-    for t in order:
-        for h in (0, 1):
-            loads[t][h].start()
+    flat_src = src_hbm.reshape(4 * s2, cells)
+    flat_pro = pro_hbm.reshape(4 * q2, cells)
+    flat_res = res_hbm.reshape(4 * q2, cells)
+
+    def third(flat, held, which):
+        return [
+            pltpu.make_async_copy(
+                flat.at[:, pl.ds(t * LANES, LANES)], held.at[t], load_sem.at[which, t]
+            )
+            for t in range(thirds)
+        ]
+
+    src_load = third(flat_src, src_raw, 0)
+    pro_load = third(flat_pro, pro_raw, 1)
+    res_load = third(flat_res, res_raw, 2)
+    for copy in (*src_load, *pro_load, *res_load):
+        copy.start()
+    for b in range(blocks):
+        loads[b].start()
 
     barrier = pltpu.get_barrier_semaphore()
     met = 0
@@ -104,6 +134,10 @@
         target = dev(sy, lax.rem(sx + d, nz))
         pl.semaphore_signal(barrier, inc=1, device_id=target, device_id_type=MESH)
         met += 1
+    for t in order:
+        src_load[t].wait()
+        for side in range(4):
+            src_ref[side, t] = src_raw[t, pl.ds(side, s2, stride=4), :]
     pl.semaphore_wait(barrier, met)
 
     lane = lax.broadcasted_iota(jnp.int32, (1, LANES), 1)
@@ -239,11 +273,35 @@
             side_copy(1, side, t).start()
     send_corners(1, lambda side, t: src_ref[side, t])
 
-    res = res_ref[...]
-    res_hi = res.astype(jnp.bfloat16)
-    res_split[0:q2] = res_hi
-    res_split[q2:] = (res - res_hi.astype(jnp.float32)).astype(jnp.bfloat16)
-    lhs[s2:rows_all] = pro_ref[...].astype(jnp.bfloat16)
+    for t in order:
+        pro_load[t].wait()
+        res_load[t].wait()
+        for side in range(4):
+            at = side * cells + t * LANES
+            lhs[s2:rows_all, at : at + LANES] = pro_raw[t, pl.ds(side, q2, stride=4), :].astype(
+                jnp.bfloat16
+            )
+            res = res_raw[t, pl.ds(side, q2, stride=4), :]
+            res_hi = res.astype(jnp.bfloat16)
+            res_split[0:q2, at : at + LANES] = res_hi
+            res_split[q2:, at : at + LANES] = (res - res_hi.astype(jnp.float32)).astype(jnp.bfloat16)
+
+    rows_i = lax.broadcasted_iota(jnp.int32, (2 * LANES, 2 * LANES), 0)
+    cols_i = lax.broadcasted_iota(jnp.int32, (2 * LANES, 2 * LANES), 1)
+    wanted = jnp.where(rows_i < LANES, 2 * rows_i, 2 * (rows_i - LANES) + 1)
+    chosen = jnp.where(cols_i == wanted, 1.0, 0.0).astype(jnp.bfloat16)
+    for b in range(blocks):
+        loads[b].wait()
+        parted = dot(chosen, raw[2 * LANES * b : 2 * LANES * (b + 1)], ((1,), (0,)))
+        parted = parted.astype(jnp.bfloat16)
+        for side in range(4):
+            h, k = side // 2, 2 * (side % 2) * LANES
+            for t in range(thirds):
+                at = side * cells + t * LANES
+                for c in (0, 1):
+                    table[t, h, b * LANES : (b + 1) * LANES, k + c * LANES : k + (c + 1) * LANES] = parted[
+                        c * LANES : (c + 1) * LANES, at : at + LANES
+                    ]
 
     def restrict(first, last):
         hi, lo = lhs[first:last], low[first:last]
@@ -289,6 +347,8 @@
                 value += jnp.where(lane == LANES - 1, ends[side][1][first:last], 0.0)
             return value
 
+        if fixed is not None and rows == s2:
+            lifted(fixed, 1)
         for t in order:
             for side in range(4):
                 side_copy(e, OUT_OF[side], t).wait_recv()
@@ -299,7 +359,7 @@
                     lift[e - 2, :, at : at + LANES] = extra
                     lhs[s2:, at : at + LANES] = hi
                     low[s2:, at : at + LANES] = (extra - hi.astype(jnp.float32)).astype(jnp.bfloat16)
-        if fixed is not None:
+        if fixed is not None and rows > s2:
             lifted(fixed, 1)
         for t in order:
             for side in range(4):
@@ -308,7 +368,7 @@
                 if fixed is not None:
                     top += fix[:, at : at + LANES]
                 if e == ITERS:
-                    out_ref[:, at : at + LANES] = top
+                    last_sum[:, at : at + LANES] = top
                     continue
                 hi = top.astype(jnp.bfloat16)
                 lhs[0:s2, at : at + LANES] = hi
@@ -328,8 +388,6 @@
             if t is None:
                 break
             for h in (0, 1):
-                if e == 2:
-                    loads[t][h].wait()
                 product = dot(lhs[0:rows], table[t, h], ((1,), (0,)))
                 for k in (0, 1):
                     side = 2 * h + k
@@ -345,12 +403,15 @@
                     side_copy(e, side, t).start()
 
     coef = {}
+    share = None
     for i in range(1, ITERS + 1):
         if i == 3:
-            sum_c(1)
             coef[1] = coarse(sum_end(1))
         elif i > 3:
-            finish(i - 2)
+            if i == 4:
+                share = sum_end(0)[:, 0:q2]
+            total = sum_end(i - 2) + dot(share, stack_of(coef[i - 3]), ((1,), (0,)), HIGH)
+            coef[i - 2] = coarse(total)
         receive(i, coef.get(i - 2))
         if i == ITERS:
             break
@@ -359,27 +420,40 @@
             half = restrict(s2, rows_all)
             start_sum(0, jnp.concatenate([half, jnp.zeros((half_q, LANES - q2), jnp.float32)], axis=1))
         multiply(i + 1)
+        if i >= 2:
+            sum_c(i - 1)
+        if i == 3:
+            sum_c(0)
         sum_b(i)
         if i == 2:
             sum_b(0)
-            sum_c(0)
-            share = sum_end(0)[:, 0:q2]
-
-            def finish(j):
-                sum_c(j)
-                total = sum_end(j) + dot(share, stack_of(coef[j - 1]), ((1,), (0,)), HIGH)
-                coef[j] = coarse(total)
-
-    finish(ITERS - 1)
+        if i == ITERS - 1:
+            sum_c(i)
+
+    total = sum_end(ITERS - 1) + dot(share, stack_of(coef[ITERS - 2]), ((1,), (0,)), HIGH)
+    coef[ITERS - 1] = coarse(total)
     lifted(coef[ITERS - 1], 0)
-    for side in range(4):
-        for t in range(thirds):
+    flat_out = out_hbm.reshape(4 * s2, cells)
+    stores = [
+        pltpu.make_async_copy(
+            src_raw.at[t], flat_out.at[:, pl.ds(t * LANES, LANES)], load_sem.at[0, t]
+        )
+        for t in range(thirds)
+    ]
+    for t in range(thirds):
+        for side in range(4):
             at = side * cells + t * LANES
-            out_ref[:, at : at + LANES] += fix[:, at : at + LANES]
-    coef_ref[...] = coef[ITERS - 1]
+            src_raw[t, pl.ds(side, s2, stride=4), :] = (
+                last_sum[:, at : at + LANES] + fix[:, at : at + LANES]
+            )
+        stores[t].start()
+    spare = jnp.zeros((LANES - half_q, s2), jnp.float32)
+    coef_ref[...] = jnp.concatenate([coef[ITERS - 1], spare], axis=0).T[:, 0:half_q]
     for a in range(ITERS):
         for stage in range(3):
             whole(a, stage).wait_send()
+    for t in range(thirds):
+        stores[t].wait()
 
 
 def solution(mesh):
@@ -395,20 +469,23 @@
         rows = s2 + q2
         depth = 4 * cells
         dims = (ny, nx, nz, s2, q2, thirds)
-        table = interface_map.reshape(depth, 2, 2, 2, thirds, LANES)
-        table = table.transpose(4, 2, 0, 3, 1, 5).reshape(thirds, 2, depth, 4 * LANES)
-        sources = source_trace.reshape(s2, 4, thirds, LANES).transpose(1, 2, 0, 3)
         chunk = width // ny
         vmem = pl.BlockSpec(memory_space=pltpu.VMEM)
+        hbm = pl.BlockSpec(memory_space=pl.ANY)
         traces, coef = pl.pallas_call(
             functools.partial(kernel, dims),
             out_shape=(
-                jax.ShapeDtypeStruct((s2, depth), jnp.float32),
-                jax.ShapeDtypeStruct((width, s2), jnp.float32),
+                jax.ShapeDtypeStruct((2, src_count, 4, cells), jnp.float32),
+                jax.ShapeDtypeStruct((s2, width), jnp.float32),
             ),
-            in_specs=[pl.BlockSpec(memory_space=pl.ANY), vmem, vmem, vmem, vmem],
-            out_specs=(vmem, vmem),
+            in_specs=[hbm, hbm, hbm, hbm, vmem],
+            out_specs=(hbm, vmem),
             scratch_shapes=[
+                pltpu.VMEM((2 * depth, depth), jnp.bfloat16),
+                pltpu.VMEM((thirds, 4 * s2, LANES), jnp.float32),
+                pltpu.VMEM((thirds, 4 * q2, LANES), jnp.float32),
+                pltpu.VMEM((thirds, 4 * q2, LANES), jnp.float32),
+                pltpu.VMEM((4, thirds, s2, LANES), jnp.float32),
                 pltpu.VMEM((thirds, 2, depth, 4 * LANES), jnp.bfloat16),
                 pltpu.VMEM((rows, depth), jnp.bfloat16),
                 pltpu.VMEM((rows, depth), jnp.bfloat16),
@@ -425,7 +502,9 @@
                 pltpu.VMEM((ITERS, chunk, LANES), jnp.float32),
                 pltpu.VMEM((ITERS, ny, chunk, LANES), jnp.float32),
                 pltpu.VMEM((s2, depth), jnp.float32),
-                pltpu.SemaphoreType.DMA((thirds, 2)),
+                pltpu.VMEM((s2, depth), jnp.float32),
+                pltpu.SemaphoreType.DMA((depth // LANES,)),
+                pltpu.SemaphoreType.DMA((3, thirds)),
                 pltpu.SemaphoreType.DMA((4, thirds)),
                 pltpu.SemaphoreType.DMA((2, 4, thirds)),
                 pltpu.SemaphoreType.DMA((2, 4)),
@@ -437,14 +516,13 @@
                 collective_id=0, has_side_effects=True, vmem_limit_bytes=60 * 1024 * 1024
             ),
         )(
-            table,
-            sources,
-            restriction.reshape(q2, depth),
-            prolongation.reshape(q2, depth),
+            interface_map.reshape(depth, 2, depth),
+            source_trace.reshape(2, src_count, 4, cells),
+            restriction.reshape(2, width, 4, cells),
+            prolongation.reshape(2, width, 4, cells),
             coarse_inverse.reshape(q2, width),
         )
-        coef = coef.reshape(width, 2, src_count).transpose(1, 2, 0)
-        return traces.reshape(source_trace.shape), coef
+        return traces.reshape(source_trace.shape), coef.reshape(2, src_count, width)
 
     where = P(("wl", "sy"), "sx", None, None, None, None)
     return jax.shard_map(

time: 164 us -> 85.7 us (0.52); the launches traced: 162 us -> 85.5 us
  local copies, waits for them, and re-layouts: 68.9 us -> 3.62 us
  Pallas kernels: 92.5 us -> 81.2 us
    transpose x1 -> x0, local copies, waits for them, and re-layouts: 23.7 us -> none  [per_device(): table.transpose(4, 2, 0, 3, 1, 5).reshape(thirds, 2, depth, 4 * LANES)]
    unnamed x9 -> x2, local copies, waits for them, and re-layouts: 25.3 us -> 3.62 us
    reshape x6 -> x0, local copies, waits for them, and re-layouts: 20 us -> none  [the longest x1 14.7 us: per_device(): table.transpose(4, 2, 0, 3, 1, 5).reshape(thirds, 2, depth, 4 * LANES)]
    pallas_call x1, Pallas kernels: 92.5 us -> 81.2 us  [per_device(): pl.pallas_call(functools.partial(kernel, dims), out_shape=(jax.ShapeDtype...]
where the time goes in v2:
time: 85.7 us; the launch traced here: 85.5 us
  Pallas kernels  81.2 us (95%)
  local copies, waits for them, and re-layouts  3.62 us (4%)
    pallas_call x1, Pallas kernels, per_device(): pl.pallas_call(functools.partial(kernel, dims), out_shape=(jax.ShapeDtype...  81.2 us
    unnamed x2, local copies, waits for them, and re-layouts  3.62 us

profile of v2, /device:TPU:32, one launch (start us, length us, event | category | flops | bytes accessed | tf_op | source)
XLA Modules:
  0.0 85.5 jit_solution(9711929940903137602)
XLA Ops:
  0.6 81.2 %shard_map.68 = (f32[2,64,4,384]{3,2,1,0:T(4,128)}, f32[128,32]{1,0:T(8,128)}) custom-call(bf16[1536,2,1536]{2,1,0:T(2,128)(2,1)} %bitcast.7, f32[2,64,4,384]{3,2,1,0:T(4,128)} %bitcast.9, f32[2,32,4,384]{3,2,1,0:T(4,128)} %bitcast.10, f32[2,32,4,384]{3,2,1,0:T(4,128)} %bitcast.11, f32[64,32]{1,0:T(8,128)} %bitcast.13), custom_call_target="tpu_custom_call" | custom-call | tf_op jit(solution)/shard_map/pallas_call | solution.py:475
  81.8 1.5 %copy.7 = f32[2,64,32]{1,2,0:T(8,128)} copy(f32[2,64,32]{2,1,0:T(8,128)} %bitcast.12) | data formatting | bytes 32768
  83.4 2.1 %copy.9 = f32[1,1,2,64,4,384]{5,4,3,2,1,0:T(4,128)} copy(f32[1,1,2,64,4,384]{5,4,3,2,1,0:T(4,128)} %bitcast.8) | data formatting | bytes 1572864

commit v3 on v2

--- a/solution.py
+++ b/solution.py
@@ -41,7 +41,9 @@
     src_ref,
     table,
     lhs,
-    low,
+    acc,
+    out_hi,
+    out_lo,
     sent,
     got,
     lift,
@@ -77,6 +79,9 @@
     def dev(row, col):
         return (row, col, wl)
 
+    def place(side, t):
+        return (order.index(t) * 4 + side) * LANES
+
     up, down = lax.rem(sy + nsy - 1, nsy), lax.rem(sy + 1, nsy)
     left, right = lax.rem(sx + nz - 1, nz), lax.rem(sx + 1, nz)
     peer = {NORTH: dev(up, sx), SOUTH: dev(down, sx), WEST: dev(sy, left), EAST: dev(sy, right)}
@@ -91,6 +96,7 @@
 
     depth = 4 * cells
     order = (0, *range(2, thirds), 1)
+    early = 4 * LANES * (thirds - 1)
     blocks = depth // LANES
     flat_map = map_hbm.reshape(2 * depth, depth)
     loads = [
@@ -136,22 +142,26 @@
         met += 1
     for t in order:
         src_load[t].wait()
+        res_load[t].wait()
         for side in range(4):
-            src_ref[side, t] = src_raw[t, pl.ds(side, s2, stride=4), :]
+            at = place(side, t)
+            value = src_raw[t, pl.ds(side, s2, stride=4), :]
+            src_ref[side, t] = value
+            sent[1, side, t, 0:s2] = value
+            sent[1, side, t, s2:] = res_raw[t, pl.ds(side, q2, stride=4), :]
     pl.semaphore_wait(barrier, met)
 
     lane = lax.broadcasted_iota(jnp.int32, (1, LANES), 1)
 
     def rows_of(e):
-        return rows_all if e in (2, 3) else s2
+        return rows_all if e <= 3 else s2
 
     def side_copy(e, side, t):
         par, rows = e % 2, rows_of(e)
-        src = src_ref.at[side, t] if e == 1 else sent.at[side, t, pl.ds(0, rows)]
         return pltpu.make_async_remote_copy(
-            src_ref=src,
+            src_ref=sent.at[par, side, t, pl.ds(0, rows)],
             dst_ref=got.at[par, OUT_OF[side], t, pl.ds(0, rows)],
-            send_sem=send_sem.at[side, t],
+            send_sem=send_sem.at[par, side, t],
             recv_sem=recv_sem.at[par, OUT_OF[side], t],
             device_id=peer[side],
             device_id_type=MESH,
@@ -271,20 +281,25 @@
     for t in order:
         for side in range(4):
             side_copy(1, side, t).start()
-    send_corners(1, lambda side, t: src_ref[side, t])
+    send_corners(1, lambda side, t: sent[1, side, t])
+
+    def split(value, side, t, first, last):
+        at = place(side, t)
+        hi = value.astype(jnp.bfloat16)
+        out_hi[first:last, at : at + LANES] = hi
+        out_lo[first:last, at : at + LANES] = (value - hi.astype(jnp.float32)).astype(jnp.bfloat16)
+
+    for t in order:
+        for side in range(4):
+            split(src_ref[side, t], side, t, 0, s2)
 
     for t in order:
         pro_load[t].wait()
-        res_load[t].wait()
         for side in range(4):
-            at = side * cells + t * LANES
+            at = place(side, t)
             lhs[s2:rows_all, at : at + LANES] = pro_raw[t, pl.ds(side, q2, stride=4), :].astype(
                 jnp.bfloat16
             )
-            res = res_raw[t, pl.ds(side, q2, stride=4), :]
-            res_hi = res.astype(jnp.bfloat16)
-            res_split[0:q2, at : at + LANES] = res_hi
-            res_split[q2:, at : at + LANES] = (res - res_hi.astype(jnp.float32)).astype(jnp.bfloat16)
 
     rows_i = lax.broadcasted_iota(jnp.int32, (2 * LANES, 2 * LANES), 0)
     cols_i = lax.broadcasted_iota(jnp.int32, (2 * LANES, 2 * LANES), 1)
@@ -298,13 +313,14 @@
             h, k = side // 2, 2 * (side % 2) * LANES
             for t in range(thirds):
                 at = side * cells + t * LANES
+                row = place(b // thirds, b % thirds)
                 for c in (0, 1):
-                    table[t, h, b * LANES : (b + 1) * LANES, k + c * LANES : k + (c + 1) * LANES] = parted[
+                    table[t, h, row : row + LANES, k + c * LANES : k + (c + 1) * LANES] = parted[
                         c * LANES : (c + 1) * LANES, at : at + LANES
                     ]
 
     def restrict(first, last):
-        hi, lo = lhs[first:last], low[first:last]
+        hi, lo = out_hi[first:last], out_lo[first:last]
         half = (last - first) // 2
         both = dot(res_split[...], hi, ((1,), (1,)))
         rest = dot(res_split[0:q2], lo, ((1,), (1,)))
@@ -319,10 +335,10 @@
     def stack_of(coef):
         return jnp.concatenate([coef, turned(coef, half_s)], axis=0)
 
-    def lifted(coef, k):
-        fix[...] = dot(stack_of(coef), lift[k], ((0,), (0,)), HIGH)
-
-    def receive(e, fixed):
+    def lifted(coef, k, first=0, last=depth):
+        fix[:, first:last] = dot(stack_of(coef), lift[k, :, first:last], ((0,), (0,)), HIGH)
+
+    def corner_columns(e):
         par, rows = e % 2, rows_of(e)
         for k in range(4):
             corner_copy(e, k).wait_recv()
@@ -337,7 +353,12 @@
         if rows > s2:
             cols = jnp.concatenate([cols, flat[0:q2, 4:8]], axis=0)
         nw, ne, sw, se = (cols[:, k : k + 1] for k in range(4))
-        ends = {NORTH: (nw, ne), SOUTH: (sw, se), WEST: (nw, sw), EAST: (ne, se)}
+        return {NORTH: (nw, ne), SOUTH: (sw, se), WEST: (nw, sw), EAST: (ne, se)}
+
+    def receive(e, some, fixed):
+        par, rows = e % 2, rows_of(e)
+        first, last = place(0, some[0]), place(0, some[-1]) + 4 * LANES
+        ends = corner_columns(e) if 0 in some else None
 
         def incoming(side, t, first, last):
             value = jnp.where(has[side], got[par, side, t, first:last], 0.0)
@@ -347,91 +368,134 @@
                 value += jnp.where(lane == LANES - 1, ends[side][1][first:last], 0.0)
             return value
 
-        if fixed is not None and rows == s2:
-            lifted(fixed, 1)
-        for t in order:
+        for t in some:
             for side in range(4):
                 side_copy(e, OUT_OF[side], t).wait_recv()
                 if rows > s2:
-                    at = side * cells + t * LANES
+                    at = place(side, t)
                     extra = incoming(side, t, s2, rows)
                     hi = extra.astype(jnp.bfloat16)
-                    lift[e - 2, :, at : at + LANES] = extra
-                    lhs[s2:, at : at + LANES] = hi
-                    low[s2:, at : at + LANES] = (extra - hi.astype(jnp.float32)).astype(jnp.bfloat16)
-        if fixed is not None and rows > s2:
-            lifted(fixed, 1)
-        for t in order:
+                    if e == 1:
+                        res_split[0:q2, at : at + LANES] = hi
+                        res_split[q2:, at : at + LANES] = (extra - hi.astype(jnp.float32)).astype(
+                            jnp.bfloat16
+                        )
+                    else:
+                        lift[e - 2, :, at : at + LANES] = extra
+                    if e == 2:
+                        lhs[s2:, at : at + LANES] = hi
+        if e == 3:
+            lifted(fixed, 1, first, last)
+        for t in some:
             for side in range(4):
-                at = side * cells + t * LANES
+                at = place(side, t)
                 top = incoming(side, t, 0, s2)
                 if fixed is not None:
                     top += fix[:, at : at + LANES]
                 if e == ITERS:
                     last_sum[:, at : at + LANES] = top
-                    continue
-                hi = top.astype(jnp.bfloat16)
-                lhs[0:s2, at : at + LANES] = hi
-                low[0:s2, at : at + LANES] = (top - hi.astype(jnp.float32)).astype(jnp.bfloat16)
+                else:
+                    lhs[0:s2, at : at + LANES] = top.astype(jnp.bfloat16)
+
+    def sends_done(e):
         for t in order:
             for side in range(4):
                 side_copy(e, side, t).wait_send()
         for k in range(4):
             corner_copy(e, k).wait_send()
 
-    def multiply(e):
-        rows = rows_of(e)
+    def multiply_early(e):
+        rows = rows_all if e in (2, 3) else s2
+        for t in order:
+            for h in (0, 1):
+                acc[t, h, 0:rows] = dot(lhs[0:rows, 0:early], table[t, h, 0:early], ((1,), (0,)))
+
+    def multiply_late(e):
+        rows, par = rows_of(e), e % 2
+        if e >= 3:
+            sends_done(e - 2)
 
         for t in (*order, None):
             if t == order[-1]:
-                send_corners(e, lambda side, t: sent[side, t, 0:rows])
+                send_corners(e, lambda side, t: sent[par, side, t, 0:rows])
             if t is None:
                 break
             for h in (0, 1):
-                product = dot(lhs[0:rows], table[t, h], ((1,), (0,)))
+                product = acc[t, h, 0:rows] + dot(
+                    lhs[0:rows, early:], table[t, h, early:], ((1,), (0,))
+                )
                 for k in (0, 1):
                     side = 2 * h + k
                     re = product[:, 2 * k * LANES : (2 * k + 1) * LANES]
                     im = product[:, (2 * k + 1) * LANES : (2 * k + 2) * LANES]
                     a, b = half_s, s2
-                    sent[side, t, 0:a] = re[0:a] - im[a:b] + src_ref[side, t, 0:a]
-                    sent[side, t, a:b] = im[0:a] + re[a:b] + src_ref[side, t, a:b]
+                    out_re = re[0:a] - im[a:b] + src_ref[side, t, 0:a]
+                    out_im = im[0:a] + re[a:b] + src_ref[side, t, a:b]
+                    sent[par, side, t, 0:a] = out_re
+                    sent[par, side, t, a:b] = out_im
+                    if e < ITERS:
+                        split(out_re, side, t, 0, a)
+                        split(out_im, side, t, a, b)
                     if rows > s2:
                         a, b = s2 + half_q, s2 + q2
-                        sent[side, t, s2:a] = re[s2:a] - im[a:b]
-                        sent[side, t, a:b] = im[s2:a] + re[a:b]
+                        out_re = re[s2:a] - im[a:b]
+                        out_im = im[s2:a] + re[a:b]
+                        sent[par, side, t, s2:a] = out_re
+                        sent[par, side, t, a:b] = out_im
+                        split(out_re, side, t, s2, a)
+                        split(out_im, side, t, a, b)
                     side_copy(e, side, t).start()
 
-    coef = {}
-    share = None
-    for i in range(1, ITERS + 1):
-        if i == 3:
-            coef[1] = coarse(sum_end(1))
-        elif i > 3:
-            if i == 4:
-                share = sum_end(0)[:, 0:q2]
-            total = sum_end(i - 2) + dot(share, stack_of(coef[i - 3]), ((1,), (0,)), HIGH)
-            coef[i - 2] = coarse(total)
-        receive(i, coef.get(i - 2))
-        if i == ITERS:
-            break
-        start_sum(i, restrict(0, s2))
-        if i == 2:
-            half = restrict(s2, rows_all)
-            start_sum(0, jnp.concatenate([half, jnp.zeros((half_q, LANES - q2), jnp.float32)], axis=1))
-        multiply(i + 1)
+    coef, share = {}, {}
+
+    def finish(j):
+        total = sum_end(j)
+        if j == 2:
+            share[0] = sum_end(0)[:, 0:q2]
+        if j == 3:
+            share[1] = sum_end(ITERS)[:, 0:q2]
+        for k in (0, 1):
+            if j - 1 - k >= 1:
+                total += dot(share[k], stack_of(coef[j - 1 - k]), ((1,), (0,)), HIGH)
+        coef[j] = coarse(total)
+
+    def lifted_rows():
+        half = restrict(s2, rows_all)
+        return jnp.concatenate([half, jnp.zeros((half_q, LANES - q2), jnp.float32)], axis=1)
+
+    for i in range(1, ITERS):
+        receive(i, order[:-1], coef.get(i - 2))
+        multiply_early(i + 1)
+        receive(i, order[-1:], coef.get(i - 2))
+        if i == 1:
+            start_sum(1, restrict(0, s2))
+        multiply_late(i + 1)
         if i >= 2:
             sum_c(i - 1)
         if i == 3:
             sum_c(0)
+        if i == 4:
+            sum_c(ITERS)
         sum_b(i)
         if i == 2:
             sum_b(0)
-        if i == ITERS - 1:
-            sum_c(i)
-
-    total = sum_end(ITERS - 1) + dot(share, stack_of(coef[ITERS - 2]), ((1,), (0,)), HIGH)
-    coef[ITERS - 1] = coarse(total)
+        if i == 3:
+            sum_b(ITERS)
+        if i < ITERS - 1:
+            start_sum(i + 1, restrict(0, s2))
+        if i == 1:
+            start_sum(0, lifted_rows())
+        if i == 2:
+            start_sum(ITERS, lifted_rows())
+        if i >= 2:
+            finish(i - 1)
+        if i >= 3:
+            lifted(coef[i - 1], 1)
+
+    receive(ITERS, order[:-1], coef[ITERS - 2])
+    receive(ITERS, order[-1:], coef[ITERS - 2])
+    sum_c(ITERS - 1)
+    finish(ITERS - 1)
     lifted(coef[ITERS - 1], 0)
     flat_out = out_hbm.reshape(4 * s2, cells)
     stores = [
@@ -442,14 +506,16 @@
     ]
     for t in range(thirds):
         for side in range(4):
-            at = side * cells + t * LANES
+            at = place(side, t)
             src_raw[t, pl.ds(side, s2, stride=4), :] = (
                 last_sum[:, at : at + LANES] + fix[:, at : at + LANES]
             )
         stores[t].start()
-    spare = jnp.zeros((LANES - half_q, s2), jnp.float32)
-    coef_ref[...] = jnp.concatenate([coef[ITERS - 1], spare], axis=0).T[:, 0:half_q]
-    for a in range(ITERS):
+    coef_ref[0] = coef[ITERS - 1][:, 0:half_s]
+    coef_ref[1] = coef[ITERS - 1][:, half_s:]
+    sends_done(ITERS - 1)
+    sends_done(ITERS)
+    for a in range(ITERS + 1):
         for stage in range(3):
             whole(a, stage).wait_send()
     for t in range(thirds):
@@ -476,7 +542,7 @@
             functools.partial(kernel, dims),
             out_shape=(
                 jax.ShapeDtypeStruct((2, src_count, 4, cells), jnp.float32),
-                jax.ShapeDtypeStruct((s2, width), jnp.float32),
+                jax.ShapeDtypeStruct((2, width, src_count), jnp.float32),
             ),
             in_specs=[hbm, hbm, hbm, hbm, vmem],
             out_specs=(hbm, vmem),
@@ -488,29 +554,31 @@
                 pltpu.VMEM((4, thirds, s2, LANES), jnp.float32),
                 pltpu.VMEM((thirds, 2, depth, 4 * LANES), jnp.bfloat16),
                 pltpu.VMEM((rows, depth), jnp.bfloat16),
+                pltpu.VMEM((thirds, 2, rows, 4 * LANES), jnp.float32),
                 pltpu.VMEM((rows, depth), jnp.bfloat16),
-                pltpu.VMEM((4, thirds, rows, LANES), jnp.float32),
+                pltpu.VMEM((rows, depth), jnp.bfloat16),
+                pltpu.VMEM((2, 4, thirds, rows, LANES), jnp.float32),
                 pltpu.VMEM((2, 4, thirds, rows, LANES), jnp.float32),
                 pltpu.VMEM((2, q2, depth), jnp.float32),
                 pltpu.VMEM((2 * q2, depth), jnp.bfloat16),
                 pltpu.VMEM((2, 8, LANES), jnp.float32),
                 pltpu.VMEM((2, 4, 8, LANES), jnp.float32),
-                pltpu.VMEM((ITERS, ny, chunk, LANES), jnp.float32),
-                pltpu.VMEM((ITERS, nsy, chunk, LANES), jnp.float32),
-                pltpu.VMEM((ITERS, chunk, LANES), jnp.float32),
-                pltpu.VMEM((ITERS, nz, chunk, LANES), jnp.float32),
-                pltpu.VMEM((ITERS, chunk, LANES), jnp.float32),
-                pltpu.VMEM((ITERS, ny, chunk, LANES), jnp.float32),
+                pltpu.VMEM((ITERS + 1, ny, chunk, LANES), jnp.float32),
+                pltpu.VMEM((ITERS + 1, nsy, chunk, LANES), jnp.float32),
+                pltpu.VMEM((ITERS + 1, chunk, LANES), jnp.float32),
+                pltpu.VMEM((ITERS + 1, nz, chunk, LANES), jnp.float32),
+                pltpu.VMEM((ITERS + 1, chunk, LANES), jnp.float32),
+                pltpu.VMEM((ITERS + 1, ny, chunk, LANES), jnp.float32),
                 pltpu.VMEM((s2, depth), jnp.float32),
                 pltpu.VMEM((s2, depth), jnp.float32),
                 pltpu.SemaphoreType.DMA((depth // LANES,)),
                 pltpu.SemaphoreType.DMA((3, thirds)),
-                pltpu.SemaphoreType.DMA((4, thirds)),
+                pltpu.SemaphoreType.DMA((2, 4, thirds)),
                 pltpu.SemaphoreType.DMA((2, 4, thirds)),
                 pltpu.SemaphoreType.DMA((2, 4)),
                 pltpu.SemaphoreType.DMA((2, 4)),
-                pltpu.SemaphoreType.DMA((ITERS, 3)),
-                pltpu.SemaphoreType.DMA((ITERS, 3)),
+                pltpu.SemaphoreType.DMA((ITERS + 1, 3)),
+                pltpu.SemaphoreType.DMA((ITERS + 1, 3)),
             ],
             compiler_params=pltpu.CompilerParams(
                 collective_id=0, has_side_effects=True, vmem_limit_bytes=60 * 1024 * 1024
@@ -522,7 +590,7 @@
             prolongation.reshape(2, width, 4, cells),
             coarse_inverse.reshape(q2, width),
         )
-        return traces.reshape(source_trace.shape), coef.reshape(2, src_count, width)
+        return traces.reshape(source_trace.shape), coef.transpose(0, 2, 1)
 
     where = P(("wl", "sy"), "sx", None, None, None, None)
     return jax.shard_map(

time: 85.7 us -> 84.8 us (0.989)
  no operation moved by 1% of the time
where the time goes in v3:
time: 84.8 us; the launch traced here: 84.5 us
  Pallas kernels  80.4 us (95%)
  local copies, waits for them, and re-layouts  3.47 us (4%)
    pallas_call x1, Pallas kernels, per_device(): pl.pallas_call(functools.partial(kernel, dims), out_shape=(jax.ShapeDtype...  80.4 us
    unnamed x2, local copies, waits for them, and re-layouts  3.47 us

profile of v3, /device:TPU:32, one launch (start us, length us, event | category | flops | bytes accessed | tf_op | source)
XLA Modules:
  0.0 84.5 jit_solution(12017987152566252401)
XLA Ops:
  0.6 80.4 %shard_map.68 = (f32[2,64,4,384]{3,2,1,0:T(4,128)}, f32[2,32,64]{2,1,0:T(8,128)}) custom-call(bf16[1536,2,1536]{2,1,0:T(2,128)(2,1)} %bitcast.7, f32[2,64,4,384]{3,2,1,0:T(4,128)} %bitcast.9, f32[2,32,4,384]{3,2,1,0:T(4,128)} %bitcast.10, f32[2,32,4,384]{3,2,1,0:T(4,128)} %bitcast.11, f32[64,32]{1,0:T(8,128)} %bitcast.12), custom_call_target="tpu_custom_call" | custom-call | tf_op jit(solution)/shard_map/pallas_call | solution.py:541
  81.0 2.1 %copy.9 = f32[1,1,2,64,4,384]{5,4,3,2,1,0:T(4,128)} copy(f32[1,1,2,64,4,384]{5,4,3,2,1,0:T(4,128)} %bitcast.8) | data formatting | bytes 1572864
  83.1 1.4 %copy.10 = f32[2,64,32]{1,2,0:T(8,128)} copy(f32[2,64,32]{1,2,0:T(8,128)} %bitcast.13) | data formatting | bytes 32768

commit v4 on v3

--- a/solution.py
+++ b/solution.py
@@ -42,6 +42,8 @@
     table,
     lhs,
     acc,
+    src_hi,
+    src_lo,
     out_hi,
     out_lo,
     sent,
@@ -62,6 +64,8 @@
     load_sem,
     send_sem,
     recv_sem,
+    wsend_sem,
+    wrecv_sem,
     csend_sem,
     crecv_sem,
     asend_sem,
@@ -154,7 +158,7 @@
     lane = lax.broadcasted_iota(jnp.int32, (1, LANES), 1)
 
     def rows_of(e):
-        return rows_all if e <= 3 else s2
+        return rows_all if e in (2, 3) else s2
 
     def side_copy(e, side, t):
         par, rows = e % 2, rows_of(e)
@@ -163,6 +167,16 @@
             dst_ref=got.at[par, OUT_OF[side], t, pl.ds(0, rows)],
             send_sem=send_sem.at[par, side, t],
             recv_sem=recv_sem.at[par, OUT_OF[side], t],
+            device_id=peer[side],
+            device_id_type=MESH,
+        )
+
+    def weight_copy(side, t):
+        return pltpu.make_async_remote_copy(
+            src_ref=sent.at[1, side, t, pl.ds(s2, q2)],
+            dst_ref=got.at[1, OUT_OF[side], t, pl.ds(s2, q2)],
+            send_sem=wsend_sem.at[side, t],
+            recv_sem=wrecv_sem.at[OUT_OF[side], t],
             device_id=peer[side],
             device_id_type=MESH,
         )
@@ -278,10 +292,13 @@
         col_in[a, 0] = col_out[a]
         return jnp.concatenate([col_in[a, lax.rem(j - yy + ny, ny)] for j in range(ny)], axis=0)
 
+    send_corners(1, lambda side, t: sent[1, side, t])
     for t in order:
         for side in range(4):
             side_copy(1, side, t).start()
-    send_corners(1, lambda side, t: sent[1, side, t])
+    for t in order:
+        for side in range(4):
+            weight_copy(side, t).start()
 
     def split(value, side, t, first, last):
         at = place(side, t)
@@ -291,7 +308,10 @@
 
     for t in order:
         for side in range(4):
-            split(src_ref[side, t], side, t, 0, s2)
+            at, value = place(side, t), src_ref[side, t]
+            hi = value.astype(jnp.bfloat16)
+            src_hi[:, at : at + LANES] = hi
+            src_lo[:, at : at + LANES] = (value - hi.astype(jnp.float32)).astype(jnp.bfloat16)
 
     for t in order:
         pro_load[t].wait()
@@ -320,8 +340,10 @@
                     ]
 
     def restrict(first, last):
-        hi, lo = out_hi[first:last], out_lo[first:last]
-        half = (last - first) // 2
+        return restricted(out_hi[first:last], out_lo[first:last])
+
+    def restricted(hi, lo):
+        half = hi.shape[0] // 2
         both = dot(res_split[...], hi, ((1,), (1,)))
         rest = dot(res_split[0:q2], lo, ((1,), (1,)))
         u = both[0:q2] + both[q2:] + rest
@@ -336,37 +358,59 @@
         return jnp.concatenate([coef, turned(coef, half_s)], axis=0)
 
     def lifted(coef, k, first=0, last=depth):
-        fix[:, first:last] = dot(stack_of(coef), lift[k, :, first:last], ((0,), (0,)), HIGH)
+        stack = stack_of(coef)
+        hi = stack.astype(jnp.bfloat16)
+        rest = (stack - hi.astype(jnp.float32)).astype(jnp.bfloat16)
+        three = jnp.concatenate([hi, hi, rest], axis=0)
+        fix[:, first:last] = dot(three, lift[k, :, first:last], ((0,), (0,)))
 
     def corner_columns(e):
         par, rows = e % 2, rows_of(e)
         for k in range(4):
             corner_copy(e, k).wait_recv()
         tile = []
-        for base in (0, 4) if rows > s2 else (0,):
+        for base in (0, 4) if e <= 3 else (0,):
             for k in range(4):
                 row = corner_in[par, k, base + 3 - k : base + 4 - k]
                 tile.append(jnp.where(has_diag[k], 0.5 * row, 0.0))
         spare = jnp.zeros((LANES - len(tile), LANES), jnp.float32)
         flat = jnp.concatenate([*tile, spare], axis=0).T
         cols = flat[:, 0:4]
-        if rows > s2:
+        if e <= 3:
             cols = jnp.concatenate([cols, flat[0:q2, 4:8]], axis=0)
         nw, ne, sw, se = (cols[:, k : k + 1] for k in range(4))
         return {NORTH: (nw, ne), SOUTH: (sw, se), WEST: (nw, sw), EAST: (ne, se)}
 
-    def receive(e, some, fixed):
+    def arrived(par, ends, side, t, first, last):
+        value = jnp.where(has[side], got[par, side, t, first:last], 0.0)
+        if t == 0:
+            value += jnp.where(lane == 0, ends[side][0][first:last], 0.0)
+        if t == thirds - 1:
+            value += jnp.where(lane == LANES - 1, ends[side][1][first:last], 0.0)
+        return value
+
+    def receive_weights(ends):
+        for t in order:
+            for side in range(4):
+                weight_copy(OUT_OF[side], t).wait_recv()
+                at = place(side, t)
+                extra = arrived(1, ends, side, t, s2, rows_all)
+                hi = extra.astype(jnp.bfloat16)
+                res_split[0:q2, at : at + LANES] = hi
+                res_split[q2:, at : at + LANES] = (extra - hi.astype(jnp.float32)).astype(
+                    jnp.bfloat16
+                )
+        for t in order:
+            for side in range(4):
+                weight_copy(side, t).wait_send()
+
+    def receive(e, some, fixed, ends=None):
         par, rows = e % 2, rows_of(e)
         first, last = place(0, some[0]), place(0, some[-1]) + 4 * LANES
-        ends = corner_columns(e) if 0 in some else None
+        ends = corner_columns(e) if ends is None else ends
 
         def incoming(side, t, first, last):
-            value = jnp.where(has[side], got[par, side, t, first:last], 0.0)
-            if t == 0:
-                value += jnp.where(lane == 0, ends[side][0][first:last], 0.0)
-            if t == thirds - 1:
-                value += jnp.where(lane == LANES - 1, ends[side][1][first:last], 0.0)
-            return value
+            return arrived(par, ends, side, t, first, last)
 
         for t in some:
             for side in range(4):
@@ -375,13 +419,10 @@
                     at = place(side, t)
                     extra = incoming(side, t, s2, rows)
                     hi = extra.astype(jnp.bfloat16)
-                    if e == 1:
-                        res_split[0:q2, at : at + LANES] = hi
-                        res_split[q2:, at : at + LANES] = (extra - hi.astype(jnp.float32)).astype(
-                            jnp.bfloat16
-                        )
-                    else:
-                        lift[e - 2, :, at : at + LANES] = extra
+                    rest = (extra - hi.astype(jnp.float32)).astype(jnp.bfloat16)
+                    lift[e - 2, 0:q2, at : at + LANES] = hi
+                    lift[e - 2, q2 : 2 * q2, at : at + LANES] = rest
+                    lift[e - 2, 2 * q2 :, at : at + LANES] = hi
                     if e == 2:
                         lhs[s2:, at : at + LANES] = hi
         if e == 3:
@@ -396,6 +437,7 @@
                     last_sum[:, at : at + LANES] = top
                 else:
                     lhs[0:s2, at : at + LANES] = top.astype(jnp.bfloat16)
+        return ends
 
     def sends_done(e):
         for t in order:
@@ -464,37 +506,41 @@
         return jnp.concatenate([half, jnp.zeros((half_q, LANES - q2), jnp.float32)], axis=1)
 
     for i in range(1, ITERS):
-        receive(i, order[:-1], coef.get(i - 2))
+        ends = receive(i, order[:-1], coef.get(i - 2))
         multiply_early(i + 1)
-        receive(i, order[-1:], coef.get(i - 2))
-        if i == 1:
-            start_sum(1, restrict(0, s2))
-        multiply_late(i + 1)
         if i >= 2:
-            sum_c(i - 1)
-        if i == 3:
-            sum_c(0)
-        if i == 4:
-            sum_c(ITERS)
-        sum_b(i)
+            sum_b(i)
         if i == 2:
             sum_b(0)
         if i == 3:
             sum_b(ITERS)
+        receive(i, order[-1:], coef.get(i - 2), ends)
+        if i == 1:
+            receive_weights(ends)
+            start_sum(1, restricted(src_hi[...], src_lo[...]))
+        multiply_late(i + 1)
+        if i == 2:
+            sum_c(1)
         if i < ITERS - 1:
             start_sum(i + 1, restrict(0, s2))
         if i == 1:
             start_sum(0, lifted_rows())
+            sum_b(1)
         if i == 2:
             start_sum(ITERS, lifted_rows())
+        if i >= 3:
+            finish(i - 1)
+            lifted(coef[i - 1], 1)
         if i >= 2:
-            finish(i - 1)
-        if i >= 3:
-            lifted(coef[i - 1], 1)
-
-    receive(ITERS, order[:-1], coef[ITERS - 2])
-    receive(ITERS, order[-1:], coef[ITERS - 2])
-    sum_c(ITERS - 1)
+            sum_c(i)
+        if i == 2:
+            sum_c(0)
+            finish(1)
+        if i == 3:
+            sum_c(ITERS)
+
+    ends = receive(ITERS, order[:-1], coef[ITERS - 2])
+    receive(ITERS, order[-1:], coef[ITERS - 2], ends)
     finish(ITERS - 1)
     lifted(coef[ITERS - 1], 0)
     flat_out = out_hbm.reshape(4 * s2, cells)
@@ -555,11 +601,13 @@
                 pltpu.VMEM((thirds, 2, depth, 4 * LANES), jnp.bfloat16),
                 pltpu.VMEM((rows, depth), jnp.bfloat16),
                 pltpu.VMEM((thirds, 2, rows, 4 * LANES), jnp.float32),
+                pltpu.VMEM((s2, depth), jnp.bfloat16),
+                pltpu.VMEM((s2, depth), jnp.bfloat16),
                 pltpu.VMEM((rows, depth), jnp.bfloat16),
                 pltpu.VMEM((rows, depth), jnp.bfloat16),
                 pltpu.VMEM((2, 4, thirds, rows, LANES), jnp.float32),
                 pltpu.VMEM((2, 4, thirds, rows, LANES), jnp.float32),
-                pltpu.VMEM((2, q2, depth), jnp.float32),
+                pltpu.VMEM((2, 3 * q2, depth), jnp.bfloat16),
                 pltpu.VMEM((2 * q2, depth), jnp.bfloat16),
                 pltpu.VMEM((2, 8, LANES), jnp.float32),
                 pltpu.VMEM((2, 4, 8, LANES), jnp.float32),
@@ -575,6 +623,8 @@
                 pltpu.SemaphoreType.DMA((3, thirds)),
                 pltpu.SemaphoreType.DMA((2, 4, thirds)),
                 pltpu.SemaphoreType.DMA((2, 4, thirds)),
+                pltpu.SemaphoreType.DMA((4, thirds)),
+                pltpu.SemaphoreType.DMA((4, thirds)),
                 pltpu.SemaphoreType.DMA((2, 4)),
                 pltpu.SemaphoreType.DMA((2, 4)),
                 pltpu.SemaphoreType.DMA((ITERS + 1, 3)),

time: 84.8 us -> 78.5 us (0.926); the launches traced: 84.5 us -> 77.2 us
  Pallas kernels: 80.4 us -> 73.1 us
    pallas_call x1, Pallas kernels: 80.4 us -> 73.1 us  [per_device(): pl.pallas_call(functools.partial(kernel, dims), out_shape=(jax.ShapeDtype...]
where the time goes in v4:
time: 78.5 us; the launch traced here: 77.2 us
  Pallas kernels  73.1 us (93%)
  local copies, waits for them, and re-layouts  3.47 us (4%)
    pallas_call x1, Pallas kernels, per_device(): pl.pallas_call(functools.partial(kernel, dims), out_shape=(jax.ShapeDtype...  73.1 us
    unnamed x2, local copies, waits for them, and re-layouts  3.47 us

profile of v4, /device:TPU:32, one launch (start us, length us, event | category | flops | bytes accessed | tf_op | source)
XLA Modules:
  0.0 77.2 jit_solution(13764731751852319011)
XLA Ops:
  0.6 73.1 %shard_map.68 = (f32[2,64,4,384]{3,2,1,0:T(4,128)}, f32[2,32,64]{2,1,0:T(8,128)}) custom-call(bf16[1536,2,1536]{2,1,0:T(2,128)(2,1)} %bitcast.7, f32[2,64,4,384]{3,2,1,0:T(4,128)} %bitcast.9, f32[2,32,4,384]{3,2,1,0:T(4,128)} %bitcast.10, f32[2,32,4,384]{3,2,1,0:T(4,128)} %bitcast.11, f32[64,32]{1,0:T(8,128)} %bitcast.12), custom_call_target="tpu_custom_call" | custom-call | tf_op jit(solution)/shard_map/pallas_call | solution.py:587
  73.7 2.1 %copy.9 = f32[1,1,2,64,4,384]{5,4,3,2,1,0:T(4,128)} copy(f32[1,1,2,64,4,384]{5,4,3,2,1,0:T(4,128)} %bitcast.8) | data formatting | bytes 1572864
  75.8 1.4 %copy.10 = f32[2,64,32]{1,2,0:T(8,128)} copy(f32[2,64,32]{1,2,0:T(8,128)} %bitcast.13) | data formatting | bytes 32768

commit v5 on v4

--- a/solution.py
+++ b/solution.py
@@ -50,6 +50,9 @@
     got,
     lift,
     res_split,
+    corner_table,
+    corner_acc,
+    corner_src,
     corner_out,
     corner_in,
     part,
@@ -192,16 +195,18 @@
             device_id_type=MESH,
         )
 
-    def send_corners(e, block):
+    def source_corners(block):
         last = thirds - 1
         n0, n1 = block(NORTH, 0)[:, 0:1], block(NORTH, last)[:, LANES - 1 :]
         s0, s1 = block(SOUTH, 0)[:, 0:1], block(SOUTH, last)[:, LANES - 1 :]
         w0, w1 = block(WEST, 0)[:, 0:1], block(WEST, last)[:, LANES - 1 :]
         e0, e1 = block(EAST, 0)[:, 0:1], block(EAST, last)[:, LANES - 1 :]
         nw, ne, sw, se = n0 + w0, n1 + e0, s0 + w1, s1 + e1
-        z = jnp.where(
+        return jnp.where(
             lane == 0, nw, jnp.where(lane == 1, ne, jnp.where(lane == 2, sw, se))
         )
+
+    def send_corners(e, z):
         first = z[0:LANES].T[0:4]
         if z.shape[0] > s2:
             spare = jnp.zeros((2 * LANES - z.shape[0], LANES), jnp.float32)
@@ -292,7 +297,9 @@
         col_in[a, 0] = col_out[a]
         return jnp.concatenate([col_in[a, lax.rem(j - yy + ny, ny)] for j in range(ny)], axis=0)
 
-    send_corners(1, lambda side, t: sent[1, side, t])
+    corners = source_corners(lambda side, t: sent[1, side, t])
+    corner_src[...] = corners[0:s2]
+    send_corners(1, corners)
     for t in order:
         for side in range(4):
             side_copy(1, side, t).start()
@@ -325,15 +332,33 @@
     cols_i = lax.broadcasted_iota(jnp.int32, (2 * LANES, 2 * LANES), 1)
     wanted = jnp.where(rows_i < LANES, 2 * rows_i, 2 * (rows_i - LANES) + 1)
     chosen = jnp.where(cols_i == wanted, 1.0, 0.0).astype(jnp.bfloat16)
+    corner_ends = (
+        ((NORTH, 0), (WEST, 0)),
+        ((NORTH, 1), (EAST, 0)),
+        ((SOUTH, 0), (WEST, 1)),
+        ((SOUTH, 1), (EAST, 1)),
+    )
     for b in range(blocks):
         loads[b].wait()
-        parted = dot(chosen, raw[2 * LANES * b : 2 * LANES * (b + 1)], ((1,), (0,)))
-        parted = parted.astype(jnp.bfloat16)
+        exact = dot(chosen, raw[2 * LANES * b : 2 * LANES * (b + 1)], ((1,), (0,)))
+        row = place(b // thirds, b % thirds)
+        picked = jnp.zeros((LANES, LANES), jnp.float32)
+        for c in (0, 1):
+            for j in (0, 1):
+                for k in range(4):
+                    side, end = corner_ends[k][j]
+                    at = side * cells + end * (thirds - 1) * LANES
+                    goal = c * 8 + j * 4 + k
+                    moved = pltpu.roll(
+                        exact[c * LANES : (c + 1) * LANES, at : at + LANES], (goal + end) % LANES, 1
+                    )
+                    picked = jnp.where(lane == goal, moved, picked)
+        corner_table[row : row + LANES] = picked.astype(jnp.bfloat16)
+        parted = exact.astype(jnp.bfloat16)
         for side in range(4):
             h, k = side // 2, 2 * (side % 2) * LANES
             for t in range(thirds):
                 at = side * cells + t * LANES
-                row = place(b // thirds, b % thirds)
                 for c in (0, 1):
                     table[t, h, row : row + LANES, k + c * LANES : k + (c + 1) * LANES] = parted[
                         c * LANES : (c + 1) * LANES, at : at + LANES
@@ -447,7 +472,8 @@
             corner_copy(e, k).wait_send()
 
     def multiply_early(e):
-        rows = rows_all if e in (2, 3) else s2
+        rows = rows_of(e)
+        corner_acc[0:rows] = dot(lhs[0:rows, 0:early], corner_table[0:early], ((1,), (0,)))
         for t in order:
             for h in (0, 1):
                 acc[t, h, 0:rows] = dot(lhs[0:rows, 0:early], table[t, h, 0:early], ((1,), (0,)))
@@ -457,11 +483,20 @@
         if e >= 3:
             sends_done(e - 2)
 
-        for t in (*order, None):
-            if t == order[-1]:
-                send_corners(e, lambda side, t: sent[par, side, t, 0:rows])
-            if t is None:
-                break
+        z = corner_acc[0:rows] + dot(lhs[0:rows, early:], corner_table[early:], ((1,), (0,)))
+        re = z + pltpu.roll(z, LANES - 4, 1)
+        im = pltpu.roll(re, LANES - 8, 1)
+        a, b = half_s, s2
+        parts = [
+            re[0:a] - im[a:b] + corner_src[0:a],
+            im[0:a] + re[a:b] + corner_src[a:b],
+        ]
+        if rows > s2:
+            a, b = s2 + half_q, s2 + q2
+            parts += [re[s2:a] - im[a:b], im[s2:a] + re[a:b]]
+        send_corners(e, jnp.concatenate(parts, axis=0))
+
+        for t in order:
             for h in (0, 1):
                 product = acc[t, h, 0:rows] + dot(
                     lhs[0:rows, early:], table[t, h, early:], ((1,), (0,))
@@ -609,6 +644,9 @@
                 pltpu.VMEM((2, 4, thirds, rows, LANES), jnp.float32),
                 pltpu.VMEM((2, 3 * q2, depth), jnp.bfloat16),
                 pltpu.VMEM((2 * q2, depth), jnp.bfloat16),
+                pltpu.VMEM((depth, LANES), jnp.bfloat16),
+                pltpu.VMEM((rows, LANES), jnp.float32),
+                pltpu.VMEM((s2, LANES), jnp.float32),
                 pltpu.VMEM((2, 8, LANES), jnp.float32),
                 pltpu.VMEM((2, 4, 8, LANES), jnp.float32),
                 pltpu.VMEM((ITERS + 1, ny, chunk, LANES), jnp.float32),

time: 78.5 us -> 77.1 us (0.982); the launches traced: 77.2 us -> 76.7 us
  no operation moved by 1% of the time
where the time goes in v5:
time: 77.1 us; the launch traced here: 76.7 us
  Pallas kernels  72.6 us (94%)
  local copies, waits for them, and re-layouts  3.47 us (5%)
    pallas_call x1, Pallas kernels, per_device(): pl.pallas_call(functools.partial(kernel, dims), out_shape=(jax.ShapeDtype...  72.6 us
    unnamed x2, local copies, waits for them, and re-layouts  3.47 us

profile of v5, /device:TPU:32, one launch (start us, length us, event | category | flops | bytes accessed | tf_op | source)
XLA Modules:
  0.0 76.7 jit_solution(8417506432723934098)
XLA Ops:
  0.6 72.6 %shard_map.68 = (f32[2,64,4,384]{3,2,1,0:T(4,128)}, f32[2,32,64]{2,1,0:T(8,128)}) custom-call(bf16[1536,2,1536]{2,1,0:T(2,128)(2,1)} %bitcast.7, f32[2,64,4,384]{3,2,1,0:T(4,128)} %bitcast.9, f32[2,32,4,384]{3,2,1,0:T(4,128)} %bitcast.10, f32[2,32,4,384]{3,2,1,0:T(4,128)} %bitcast.11, f32[64,32]{1,0:T(8,128)} %bitcast.12), custom_call_target="tpu_custom_call" | custom-call | tf_op jit(solution)/shard_map/pallas_call | solution.py:622
  73.3 2.1 %copy.9 = f32[1,1,2,64,4,384]{5,4,3,2,1,0:T(4,128)} copy(f32[1,1,2,64,4,384]{5,4,3,2,1,0:T(4,128)} %bitcast.8) | data formatting | bytes 1572864
  75.4 1.4 %copy.10 = f32[2,64,32]{1,2,0:T(8,128)} copy(f32[2,64,32]{1,2,0:T(8,128)} %bitcast.13) | data formatting | bytes 32768

commit v6 on v5

--- a/solution.py
+++ b/solution.py
@@ -31,8 +31,10 @@
     src_hbm,
     res_hbm,
     pro_hbm,
+    inv_hbm,
+    out_hbm,
+    coef_hbm,
     inv_ref,
-    out_hbm,
     coef_ref,
     raw,
     src_raw,
@@ -65,6 +67,7 @@
     last_sum,
     map_sem,
     load_sem,
+    small_sem,
     send_sem,
     recv_sem,
     wsend_sem,
@@ -129,7 +132,9 @@
     src_load = third(flat_src, src_raw, 0)
     pro_load = third(flat_pro, pro_raw, 1)
     res_load = third(flat_res, res_raw, 2)
-    for copy in (*src_load, *pro_load, *res_load):
+    inv_load = pltpu.make_async_copy(inv_hbm, inv_ref, small_sem.at[0])
+    coef_store = pltpu.make_async_copy(coef_ref, coef_hbm, small_sem.at[1])
+    for copy in (*src_load, *res_load, *pro_load, inv_load):
         copy.start()
     for b in range(blocks):
         loads[b].start()
@@ -320,6 +325,7 @@
             src_hi[:, at : at + LANES] = hi
             src_lo[:, at : at + LANES] = (value - hi.astype(jnp.float32)).astype(jnp.bfloat16)
 
+    inv_load.wait()
     for t in order:
         pro_load[t].wait()
         for side in range(4):
@@ -478,7 +484,7 @@
             for h in (0, 1):
                 acc[t, h, 0:rows] = dot(lhs[0:rows, 0:early], table[t, h, 0:early], ((1,), (0,)))
 
-    def multiply_late(e):
+    def multiply_late(e, sums):
         rows, par = rows_of(e), e % 2
         if e >= 3:
             sends_done(e - 2)
@@ -497,6 +503,9 @@
         send_corners(e, jnp.concatenate(parts, axis=0))
 
         for t in order:
+            if t == order[-1]:
+                for a in sums:
+                    sum_b(a)
             for h in (0, 1):
                 product = acc[t, h, 0:rows] + dot(
                     lhs[0:rows, early:], table[t, h, early:], ((1,), (0,))
@@ -543,17 +552,19 @@
     for i in range(1, ITERS):
         ends = receive(i, order[:-1], coef.get(i - 2))
         multiply_early(i + 1)
-        if i >= 2:
+        if i == ITERS - 1:
             sum_b(i)
-        if i == 2:
-            sum_b(0)
+        if i >= 3:
+            sum_c(i - 1)
         if i == 3:
-            sum_b(ITERS)
+            sum_c(0)
+        if i == 4:
+            sum_c(ITERS)
         receive(i, order[-1:], coef.get(i - 2), ends)
         if i == 1:
             receive_weights(ends)
             start_sum(1, restricted(src_hi[...], src_lo[...]))
-        multiply_late(i + 1)
+        multiply_late(i + 1, {2: (2, 0), 3: (3, ITERS), 4: (4,)}.get(i, ()))
         if i == 2:
             sum_c(1)
         if i < ITERS - 1:
@@ -563,20 +574,19 @@
             sum_b(1)
         if i == 2:
             start_sum(ITERS, lifted_rows())
+            finish(1)
         if i >= 3:
             finish(i - 1)
             lifted(coef[i - 1], 1)
-        if i >= 2:
+        if i == ITERS - 1:
             sum_c(i)
-        if i == 2:
-            sum_c(0)
-            finish(1)
-        if i == 3:
-            sum_c(ITERS)
 
     ends = receive(ITERS, order[:-1], coef[ITERS - 2])
     receive(ITERS, order[-1:], coef[ITERS - 2], ends)
     finish(ITERS - 1)
+    coef_ref[0] = coef[ITERS - 1][:, 0:half_s]
+    coef_ref[1] = coef[ITERS - 1][:, half_s:]
+    coef_store.start()
     lifted(coef[ITERS - 1], 0)
     flat_out = out_hbm.reshape(4 * s2, cells)
     stores = [
@@ -592,8 +602,6 @@
                 last_sum[:, at : at + LANES] + fix[:, at : at + LANES]
             )
         stores[t].start()
-    coef_ref[0] = coef[ITERS - 1][:, 0:half_s]
-    coef_ref[1] = coef[ITERS - 1][:, half_s:]
     sends_done(ITERS - 1)
     sends_done(ITERS)
     for a in range(ITERS + 1):
@@ -601,6 +609,7 @@
             whole(a, stage).wait_send()
     for t in range(thirds):
         stores[t].wait()
+    coef_store.wait()
 
 
 def solution(mesh):
@@ -617,7 +626,6 @@
         depth = 4 * cells
         dims = (ny, nx, nz, s2, q2, thirds)
         chunk = width // ny
-        vmem = pl.BlockSpec(memory_space=pltpu.VMEM)
         hbm = pl.BlockSpec(memory_space=pl.ANY)
         traces, coef = pl.pallas_call(
             functools.partial(kernel, dims),
@@ -625,9 +633,11 @@
                 jax.ShapeDtypeStruct((2, src_count, 4, cells), jnp.float32),
                 jax.ShapeDtypeStruct((2, width, src_count), jnp.float32),
             ),
-            in_specs=[hbm, hbm, hbm, hbm, vmem],
-            out_specs=(hbm, vmem),
+            in_specs=[hbm] * 5,
+            out_specs=(hbm, hbm),
             scratch_shapes=[
+                pltpu.VMEM((q2, width), jnp.float32),
+                pltpu.VMEM((2, width, src_count), jnp.float32),
                 pltpu.VMEM((2 * depth, depth), jnp.bfloat16),
                 pltpu.VMEM((thirds, 4 * s2, LANES), jnp.float32),
                 pltpu.VMEM((thirds, 4 * q2, LANES), jnp.float32),
@@ -659,6 +669,7 @@
                 pltpu.VMEM((s2, depth), jnp.float32),
                 pltpu.SemaphoreType.DMA((depth // LANES,)),
                 pltpu.SemaphoreType.DMA((3, thirds)),
+                pltpu.SemaphoreType.DMA((2,)),
                 pltpu.SemaphoreType.DMA((2, 4, thirds)),
                 pltpu.SemaphoreType.DMA((2, 4, thirds)),
                 pltpu.SemaphoreType.DMA((4, thirds)),

time: 77.1 us -> 76.6 us (level)
  Pallas kernels: 72.6 us -> 71.4 us
    pallas_call x1, Pallas kernels: 72.6 us -> 71.4 us  [per_device(): pl.pallas_call(functools.partial(kernel, dims), out_shape=(jax.ShapeDtype...]
where the time goes in v6:
time: 76.6 us; the launch traced here: 75.5 us
  Pallas kernels  71.4 us (93%)
  local copies, waits for them, and re-layouts  3.47 us (5%)
    pallas_call x1, Pallas kernels, per_device(): pl.pallas_call(functools.partial(kernel, dims), out_shape=(jax.ShapeDtype...  71.4 us
    unnamed x2, local copies, waits for them, and re-layouts  3.47 us

profile of v6, /device:TPU:32, one launch (start us, length us, event | category | flops | bytes accessed | tf_op | source)
XLA Modules:
  0.0 75.5 jit_solution(17551372481488848402)
XLA Ops:
  0.6 71.4 %shard_map.68 = (f32[2,64,4,384]{3,2,1,0:T(4,128)}, f32[2,32,64]{2,1,0:T(8,128)}) custom-call(bf16[1536,2,1536]{2,1,0:T(2,128)(2,1)} %bitcast.7, f32[2,64,4,384]{3,2,1,0:T(4,128)} %bitcast.9, f32[2,32,4,384]{3,2,1,0:T(4,128)} %bitcast.10, f32[2,32,4,384]{3,2,1,0:T(4,128)} %bitcast.11, f32[64,32]{1,0:T(8,128)} %bitcast.12), custom_call_target="tpu_custom_call" | custom-call | tf_op jit(solution)/shard_map/pallas_call | solution.py:630
  72.0 2.1 %copy.9 = f32[1,1,2,64,4,384]{5,4,3,2,1,0:T(4,128)} copy(f32[1,1,2,64,4,384]{5,4,3,2,1,0:T(4,128)} %bitcast.8) | data formatting | bytes 1572864
  74.1 1.4 %copy.10 = f32[2,64,32]{1,2,0:T(8,128)} copy(f32[2,64,32]{1,2,0:T(8,128)} %bitcast.13) | data formatting | bytes 32768

commit v7 on v6

--- a/solution.py
+++ b/solution.py
@@ -610,6 +610,32 @@
     for t in range(thirds):
         stores[t].wait()
     coef_store.wait()
+
+
+def hand_over(traces_hbm, coef_hbm, out_hbm, coef_out_hbm, traces, coef, in_sem, out_sem):
+    halves, sources = traces.shape[0], traces.shape[1] // 2
+    pieces = [(c, pl.ds(k * sources, sources)) for c in range(halves) for k in (0, 1)]
+    moves = [
+        (
+            pltpu.make_async_copy(traces_hbm.at[c, d], traces.at[c, d], in_sem.at[n]),
+            pltpu.make_async_copy(traces.at[c, d], out_hbm.at[c, d], out_sem.at[n]),
+        )
+        for n, (c, d) in enumerate(pieces)
+    ]
+    n = len(pieces)
+    moves.append(
+        (
+            pltpu.make_async_copy(coef_hbm, coef, in_sem.at[n]),
+            pltpu.make_async_copy(coef, coef_out_hbm, out_sem.at[n]),
+        )
+    )
+    for load, _ in moves:
+        load.start()
+    for load, store in moves:
+        load.wait()
+        store.start()
+    for _, store in moves:
+        store.wait()
 
 
 def solution(mesh):
@@ -689,6 +715,21 @@
             prolongation.reshape(2, width, 4, cells),
             coarse_inverse.reshape(q2, width),
         )
+        traces, coef = pl.pallas_call(
+            hand_over,
+            out_shape=(
+                jax.ShapeDtypeStruct(traces.shape, traces.dtype),
+                jax.ShapeDtypeStruct(coef.shape, coef.dtype),
+            ),
+            in_specs=[hbm, hbm],
+            out_specs=(hbm, hbm),
+            scratch_shapes=[
+                pltpu.VMEM(traces.shape, traces.dtype),
+                pltpu.VMEM(coef.shape, coef.dtype),
+                pltpu.SemaphoreType.DMA((5,)),
+                pltpu.SemaphoreType.DMA((5,)),
+            ],
+        )(traces, coef)
         return traces.reshape(source_trace.shape), coef.transpose(0, 2, 1)
 
     where = P(("wl", "sy"), "sx", None, None, None, None)

time: 76.6 us -> 75.1 us (0.980)
  local copies, waits for them, and re-layouts: 3.47 us -> 0 us
  Pallas kernels: 71.4 us -> 73.3 us
    unnamed x2 -> x0, local copies, waits for them, and re-layouts: 3.47 us -> none
    pallas_call x0 -> x1, Pallas kernels: none -> 1.99 us  [per_device(): pl.pallas_call(hand_over, out_shape=(jax.ShapeDtypeStruct(traces.shape, t...]
where the time goes in v7:
time: 75.1 us; the launch traced here: 74.1 us
  Pallas kernels  73.3 us (98%)
  between operations  0.8 us (1%)
    pallas_call x1, Pallas kernels, per_device(): pl.pallas_call(functools.partial(kernel, dims), out_shape=(jax.ShapeDtype...  71.4 us
    pallas_call x1, Pallas kernels, per_device(): pl.pallas_call(hand_over, out_shape=(jax.ShapeDtypeStruct(traces.shape, t...  1.99 us

profile of v7, /device:TPU:32, one launch (start us, length us, event | category | flops | bytes accessed | tf_op | source)
XLA Modules:
  0.0 74.1 jit_solution(12161501956759216600)
XLA Ops:
  0.6 71.4 %shard_map.68 = (f32[2,64,4,384]{3,2,1,0:T(4,128)}, f32[2,32,64]{2,1,0:T(8,128)}) custom-call(bf16[1536,2,1536]{2,1,0:T(2,128)(2,1)} %bitcast.7, f32[2,64,4,384]{3,2,1,0:T(4,128)} %bitcast.8, f32[2,32,4,384]{3,2,1,0:T(4,128)} %bitcast.9, f32[2,32,4,384]{3,2,1,0:T(4,128)} %bitcast.10, f32[64,32]{1,0:T(8,128)} %bitcast.11), custom_call_target="tpu_custom_call" | custom-call | tf_op jit(solution)/shard_map/pallas_call | solution.py:656
  72.0 2.0 %shard_map.69 = (f32[2,64,4,384]{3,2,1,0:T(4,128)}, f32[2,32,64]{2,1,0:T(8,128)}) custom-call(f32[2,64,4,384]{3,2,1,0:T(4,128)} %get-tuple-element.6.traces_hbm, f32[2,32,64]{2,1,0:T(8,128)} %get-tuple-element.7.coef_hbm), custom_call_target="tpu_custom_call" | custom-call | tf_op jit(solution)/shard_map/pallas_call | solution.py:718
